TPU v7x, 256 devices: a whole 4x4x8 slice. The times are simulated.
256 devices in a mesh: row: 32 (over y, z), col: 8 (over x, core).
Axes of the slice: x: 4, y: 4, z: 8, core: 2. Of those that a mesh axis runs over, the one named last changes fastest.
Arguments:
- eigvecs: float32 [131072, 1024], P('row', 'col'), may hold values from -6 to 6
- reflectors: float32 [4, 131072, 256], P(None, ('row', 'col'))
- factors: float32 [4, 256, 256], replicated, as said below
Outputs:
- transformed: float32 [131072, 1024], P('row', 'col')
Inputs may be any that keep to these rules, and one draw needn't show every extreme that they name: Each factors[k] is upper triangular with a positive diagonal.
All inputs are finite; a program needn't handle non-finite values.
Results may differ from a plain program's by a relative error of at most 0.00012.
Values sent between devices are 32-bit elements; how exact they have to be, the bound alone decides.
No kernel may reach another device: no remote copies, remote signals or barrier semaphores. Data moves between devices by JAX's collectives and lax.ppermute only.
A program may use at most 128 MiB of HBM per device.

v0:
```python
import jax
import jax.numpy as jnp
from jax import lax
from jax.sharding import Mesh
from jax.sharding import PartitionSpec as P

COL = ("col_0", "col_1")
ROW_COL = ("row", "col_0", "col_1")


def copy_for_each(x, axis):
    copies = jnp.broadcast_to(x, (lax.axis_size(axis), *x.shape))
    return lax.all_to_all(copies, axis, split_axis=0, concat_axis=0, tiled=True)


def joined_along(tiles, dim):
    dims = list(tiles.shape[1:])
    dims[dim] *= tiles.shape[0]
    return jnp.moveaxis(tiles, 0, dim).reshape(dims)


def whole_of(x, axes, dim):
    far, near = axes
    leading = copy_for_each(x, far)
    tiles = jnp.swapaxes(copy_for_each(leading, near), 0, 1)
    return joined_along(tiles.reshape(-1, *x.shape), dim)


def padded_to(lines, peers):
    spare = -lines.shape[0] % peers
    if not spare:
        return lines
    return jnp.concatenate([lines, jnp.zeros((spare, *lines.shape[1:]), lines.dtype)])


def gathered_copies(x, axis, dim):
    return joined_along(copy_for_each(x, axis), dim)


def split_up(x, dim, peers):
    dims = x.shape
    tiles = x.reshape(*dims[:dim], peers, dims[dim] // peers, *dims[dim + 1 :])
    return jnp.moveaxis(tiles, dim, 0)


def summed_on_arrival(x, axis, dim):
    tiles = split_up(x, dim, lax.axis_size(axis))
    arrived = lax.all_to_all(tiles, axis, split_axis=0, concat_axis=0, tiled=True)
    return arrived.sum(axis=0)


def total_of(x, axes):
    lines = x.reshape(-1, x.shape[-1])
    padded = padded_to(lines, lax.axis_size(axes))
    whole = gathered_copies(summed_on_arrival(padded, axes, 0), axes, 0)
    return lax.slice_in_dim(whole, 0, len(lines)).reshape(x.shape)


def product(left, right):
    return jnp.dot(left, right, precision=lax.Precision.HIGHEST, preferred_element_type=jnp.float32)


def inner(left, right):
    return lax.dot_general(
        left,
        right,
        (((0,), (0,)), ((), ())),
        precision=lax.Precision.HIGHEST,
        preferred_element_type=jnp.float32,
    )


def keep_same(parts):
    return parts


def apply_panels(field, factors, fetch, reduce_value, spread):
    panels = factors.shape[0]
    for index in range(panels):
        vectors = fetch(index)
        sums = reduce_value((inner(vectors, field),))
        coeffs = product(factors[index], sums[0])
        field = field - product(vectors, spread((coeffs,))[0])
    return field


def body(eigvecs, reflectors, factors):

    def fetch(index):
        return whole_of(reflectors[index], ("col_0", "col_1"), 0)

    def reduce_value(parts):
        return jax.tree.map(lambda part: total_of(part, "row"), parts)

    return apply_panels(eigvecs, factors, fetch, reduce_value, keep_same)


def solution(mesh):
    split = Mesh(mesh.devices.reshape(mesh.shape["row"], 4, 2), ("row", "col_0", "col_1"))
    in_specs = (P("row", COL), P(None, ROW_COL, None), P())
    out_specs = P("row", COL)
    return jax.shard_map(body, mesh=split, in_specs=in_specs, out_specs=out_specs, check_vma=False)
```

profile of v0, /device:TPU:32, one launch (start us, length us, event | category | flops | bytes accessed | tf_op | source)
XLA Modules:
  0.0 321.9 jit_solution(18105307061436955398)
XLA Ops:
  2.1 30.4 %all_to_all.80 = f32[4,512,256]{1,2,0:T(8,128)S(1)} all-to-all(f32[4,512,256]{1,2,0:T(8,128)S(1)} %broadcast_in_dim.36), channel_id=1, replica_groups=mesh['row'=32,'col_0'=4,'col_1'=2] {'col_0'}, dimensions={0} | all-to-all | bytes 4194304 | tf_op jit(solution)/shard_map/all_to_all | solution.py:13
  34.4 8.2 %all_to_all.81 = f32[2,4,512,256]{2,1,3,0:T(4,128)} all-to-all(f32[2,4,512,256]{2,1,3,0:T(4,128)S(1)} %broadcast_in_dim.37), channel_id=1, replica_groups=mesh['row'=32,'col_0'=4,'col_1'=2] {'col_1'}, dimensions={0} | all-to-all | bytes 8388608 | tf_op jit(solution)/shard_map/all_to_all | solution.py:13
  48.6 5.3 %copy.25 = f32[2,4,512,256]{3,2,0,1:T(8,128)} copy(f32[2,4,512,256]{2,1,3,0:T(4,128)} %all_to_all.81) | data formatting | bytes 8388608 | tf_op jit(solution)/shard_map/all_to_all | solution.py:13
  53.8 5.8 %copy.26 = f32[256,4096]{1,0:T(8,128)} copy(f32[256,4096]{0,1:T(8,128)} %bitcast.95) | data formatting | bytes 8388608 | tf_op jit(solution)/shard_map/dot_general | solution.py:64
  59.7 5.9 %fusion.4 = f32[32,8,128]{2,1,0:T(8,128)S(1)} fusion(f32[256,4096]{1,0:T(8,128)} %copy.26, f32[4096,128]{1,0:T(8,128)S(1)} %copy-done.8), kind=kOutput, calls=%fused_computation.8 | convolution fusion | flops 1610612736 | bytes 6422528 | tf_op jit(solution)/shard_map/dot_general | solution.py:64
  65.6 10.0 %all-to-all-done.4 = f32[4,512,256]{2,1,0:T(8,128)} async-done(((f32[4,512,256]{2,1,0:T(8,128)}), f32[4,512,256]{2,1,0:T(8,128)}, u32[]{:S(2)}, u32[]{:S(2)}) %all-to-all-start.4) | async-done | bytes 2097184 | tf_op jit(solution)/shard_map/all_to_all | solution.py:13
  75.5 20.9 %all_to_all.82 = f32[32,8,128]{2,1,0:T(8,128)S(1)} all-to-all(f32[32,8,128]{2,1,0:T(8,128)S(1)} %fusion.4), channel_id=1, replica_groups=mesh['row'=32,'col_0'=4,'col_1'=2] {'row'}, dimensions={0} | all-to-all | bytes 262144 | tf_op jit(solution)/shard_map/all_to_all | solution.py:48
  100.4 5.6 %all-to-all-start.5 = ((f32[2,4,512,256]{3,2,1,0:T(8,128)}), f32[2,4,512,256]{3,2,1,0:T(8,128)}, u32[]{:S(2)}, u32[]{:S(2)}) async-start(f32[2,4,512,256]{3,2,1,0:T(8,128)} %broadcast_in_dim.40), calls=%async_computation.5 | async-start | bytes 8388608 | tf_op jit(solution)/shard_map/all_to_all | solution.py:13
  110.5 14.1 %all_to_all.83 = f32[32,8,128]{2,1,0:T(8,128)S(1)} all-to-all(f32[32,8,128]{2,1,0:T(8,128)S(1)} %broadcast_in_dim.38), channel_id=1, replica_groups=mesh['row'=32,'col_0'=4,'col_1'=2] {'row'}, dimensions={0} | all-to-all | bytes 262144 | tf_op jit(solution)/shard_map/all_to_all | solution.py:13
  126.1 4.6 %all-to-all-start.8 = ((f32[4,512,256]{2,1,0:T(8,128)}), f32[4,512,256]{2,1,0:T(8,128)}, u32[]{:S(2)}, u32[]{:S(2)}) async-start(f32[4,512,256]{2,1,0:T(8,128)} %broadcast_in_dim.42), calls=%async_computation.8 | async-start | bytes 4194304 | tf_op jit(solution)/shard_map/all_to_all | solution.py:13
  144.6 11.3 %all-to-all-done.8 = f32[4,512,256]{2,1,0:T(8,128)} async-done(((f32[4,512,256]{2,1,0:T(8,128)}), f32[4,512,256]{2,1,0:T(8,128)}, u32[]{:S(2)}, u32[]{:S(2)}) %all-to-all-start.8) | async-done | bytes 2097184 | tf_op jit(solution)/shard_map/all_to_all | solution.py:13
  155.8 14.7 %all_to_all.84 = f32[32,8,128]{2,1,0:T(8,128)S(1)} all-to-all(f32[32,8,128]{2,1,0:T(8,128)S(1)} %bitcast.99), channel_id=1, replica_groups=mesh['row'=32,'col_0'=4,'col_1'=2] {'row'}, dimensions={0} | all-to-all | bytes 262144 | tf_op jit(solution)/shard_map/all_to_all | solution.py:48
  174.4 5.6 %all-to-all-start.9 = ((f32[2,4,512,256]{3,2,1,0:T(8,128)}), f32[2,4,512,256]{3,2,1,0:T(8,128)}, u32[]{:S(2)}, u32[]{:S(2)}) async-start(f32[2,4,512,256]{3,2,1,0:T(8,128)} %broadcast_in_dim.43), calls=%async_computation.9 | async-start | bytes 8388608 | tf_op jit(solution)/shard_map/all_to_all | solution.py:13
  184.5 14.2 %all_to_all.85 = f32[32,8,128]{2,1,0:T(8,128)S(1)} all-to-all(f32[32,8,128]{2,1,0:T(8,128)S(1)} %broadcast_in_dim.41), channel_id=1, replica_groups=mesh['row'=32,'col_0'=4,'col_1'=2] {'row'}, dimensions={0} | all-to-all | bytes 262144 | tf_op jit(solution)/shard_map/all_to_all | solution.py:13
  200.3 4.7 %all-to-all-start.12 = ((f32[4,512,256]{2,1,0:T(8,128)}), f32[4,512,256]{2,1,0:T(8,128)}, u32[]{:S(2)}, u32[]{:S(2)}) async-start(f32[4,512,256]{2,1,0:T(8,128)} %broadcast_in_dim.45), calls=%async_computation.12 | async-start | bytes 4194304 | tf_op jit(solution)/shard_map/all_to_all | solution.py:13
  216.7 13.3 %all-to-all-done.12 = f32[4,512,256]{2,1,0:T(8,128)} async-done(((f32[4,512,256]{2,1,0:T(8,128)}), f32[4,512,256]{2,1,0:T(8,128)}, u32[]{:S(2)}, u32[]{:S(2)}) %all-to-all-start.12) | async-done | bytes 2097184 | tf_op jit(solution)/shard_map/all_to_all | solution.py:13
  230.0 14.7 %all_to_all.86 = f32[32,8,128]{2,1,0:T(8,128)S(1)} all-to-all(f32[32,8,128]{2,1,0:T(8,128)S(1)} %bitcast.100), channel_id=1, replica_groups=mesh['row'=32,'col_0'=4,'col_1'=2] {'row'}, dimensions={0} | all-to-all | bytes 262144 | tf_op jit(solution)/shard_map/all_to_all | solution.py:48
  248.6 5.6 %all-to-all-start.13 = ((f32[2,4,512,256]{3,2,1,0:T(8,128)}), f32[2,4,512,256]{3,2,1,0:T(8,128)}, u32[]{:S(2)}, u32[]{:S(2)}) async-start(f32[2,4,512,256]{3,2,1,0:T(8,128)} %broadcast_in_dim.46), calls=%async_computation.13 | async-start | bytes 8388608 | tf_op jit(solution)/shard_map/all_to_all | solution.py:13
  263.9 4.6 %copy.32 = f32[2,4,512,256]{3,2,0,1:T(8,128)} copy(f32[2,4,512,256]{3,2,1,0:T(8,128)} %all-to-all-done.13) | data formatting | bytes 8388608 | tf_op jit(solution)/shard_map/all_to_all | solution.py:13
  268.4 5.8 %all-to-all-done.11 = f32[32,8,128]{2,1,0:T(8,128)S(1)} async-done(((f32[32,8,128]{2,1,0:T(8,128)}), f32[32,8,128]{2,1,0:T(8,128)S(1)}, u32[]{:S(2)}, u32[]{:S(2)}) %all-to-all-start.11) | async-done | bytes 131104 | tf_op jit(solution)/shard_map/all_to_all | solution.py:13
  274.7 6.7 %fusion.1 = f32[4096,128]{0,1:T(8,128)S(1)} fusion(f32[4096,128]{0,1:T(8,128)S(1)} %copy-done.6, f32[128,256]{1,0:T(8,128)S(1)} %fusion.9, f32[4096,256]{1,0:T(8,128)} %bitcast.94), kind=kOutput, calls=%fused_computation.3 | convolution fusion | flops 1611137024 | bytes 8519680 | tf_op jit(solution)/shard_map/dot_general | solution.py:60
  284.8 13.8 %all_to_all.87 = f32[32,8,128]{2,1,0:T(8,128)S(1)} all-to-all(f32[32,8,128]{2,1,0:T(8,128)S(1)} %bitcast.101), channel_id=1, replica_groups=mesh['row'=32,'col_0'=4,'col_1'=2] {'row'}, dimensions={0} | all-to-all | bytes 262144 | tf_op jit(solution)/shard_map/all_to_all | solution.py:48
  298.7 13.9 %all_to_all.88 = f32[32,8,128]{2,1,0:T(8,128)S(1)} all-to-all(f32[32,8,128]{2,1,0:T(8,128)S(1)} %broadcast_in_dim.47), channel_id=1, replica_groups=mesh['row'=32,'col_0'=4,'col_1'=2] {'row'}, dimensions={0} | all-to-all | bytes 262144 | tf_op jit(solution)/shard_map/all_to_all | solution.py:13
  313.0 7.1 %fusion = f32[4096,128]{0,1:T(8,128)S(1)} fusion(f32[4096,128]{0,1:T(8,128)} %copy-done.7, f32[128,256]{1,0:T(8,128)S(1)} %fusion.7, f32[4096,256]{1,0:T(8,128)} %bitcast.97), kind=kOutput, calls=%fused_computation.1 | convolution fusion | flops 1611137024 | bytes 8519680 | tf_op jit(solution)/shard_map/dot_general | solution.py:60
  (62 shorter events, 74.9 us)
Async XLA Ops:
  44.1 31.4 %all-to-all-start.4 = ((f32[4,512,256]{2,1,0:T(8,128)}), f32[4,512,256]{2,1,0:T(8,128)}, u32[]{:S(2)}, u32[]{:S(2)}) async-start(f32[4,512,256]{2,1,0:T(8,128)} %broadcast_in_dim.39), calls=%async_computation.4 | async-start | bytes 4194304 | tf_op jit(solution)/shard_map/all_to_all | solution.py:13
  53.8 5.8 %copy-start.8 = (f32[4096,128]{1,0:T(8,128)S(1)}, f32[4096,128]{1,0:T(8,128)}, u32[]{:S(2)}) copy-start(f32[4096,128]{1,0:T(8,128)} %param.3) | copy-start | bytes 6291460
  100.4 10.1 %all-to-all-start.5 = ((f32[2,4,512,256]{3,2,1,0:T(8,128)}), f32[2,4,512,256]{3,2,1,0:T(8,128)}, u32[]{:S(2)}, u32[]{:S(2)}) async-start(f32[2,4,512,256]{3,2,1,0:T(8,128)} %broadcast_in_dim.40), calls=%async_computation.5 | async-start | bytes 8388608 | tf_op jit(solution)/shard_map/all_to_all | solution.py:13
  126.1 29.7 %all-to-all-start.8 = ((f32[4,512,256]{2,1,0:T(8,128)}), f32[4,512,256]{2,1,0:T(8,128)}, u32[]{:S(2)}, u32[]{:S(2)}) async-start(f32[4,512,256]{2,1,0:T(8,128)} %broadcast_in_dim.42), calls=%async_computation.8 | async-start | bytes 4194304 | tf_op jit(solution)/shard_map/all_to_all | solution.py:13
  132.6 5.4 %copy-start.3 = (f32[2,4,512,256]{3,2,0,1:T(8,128)S(1)}, f32[2,4,512,256]{3,2,0,1:T(8,128)}, u32[]{:S(2)}) copy-start(f32[2,4,512,256]{3,2,0,1:T(8,128)} %copy.25) | copy-start | bytes 12582916
  132.6 5.4 %copy-start.9 = (f32[4096,128]{0,1:T(8,128)S(1)}, f32[4096,128]{0,1:T(8,128)}, u32[]{:S(2)}) copy-start(f32[4096,128]{0,1:T(8,128)} %copy.27) | copy-start | bytes 6291460
  135.4 7.0 %copy-start = (f32[2,4,512,256]{3,2,0,1:T(8,128)}, f32[2,4,512,256]{3,2,0,1:T(8,128)S(1)}, u32[]{:S(2)}) copy-start(f32[2,4,512,256]{3,2,0,1:T(8,128)S(1)} %copy.28) | copy-start | bytes 12582916
  174.4 10.1 %all-to-all-start.9 = ((f32[2,4,512,256]{3,2,1,0:T(8,128)}), f32[2,4,512,256]{3,2,1,0:T(8,128)}, u32[]{:S(2)}, u32[]{:S(2)}) async-start(f32[2,4,512,256]{3,2,1,0:T(8,128)} %broadcast_in_dim.43), calls=%async_computation.9 | async-start | bytes 8388608 | tf_op jit(solution)/shard_map/all_to_all | solution.py:13
  200.3 29.7 %all-to-all-start.12 = ((f32[4,512,256]{2,1,0:T(8,128)}), f32[4,512,256]{2,1,0:T(8,128)}, u32[]{:S(2)}, u32[]{:S(2)}) async-start(f32[4,512,256]{2,1,0:T(8,128)} %broadcast_in_dim.45), calls=%async_computation.12 | async-start | bytes 4194304 | tf_op jit(solution)/shard_map/all_to_all | solution.py:13
  205.0 2.8 copy-start.10
  205.0 3.8 %copy-start.1 = (f32[2,4,512,256]{3,2,0,1:T(8,128)S(1)}, f32[2,4,512,256]{3,2,0,1:T(8,128)}, u32[]{:S(2)}) copy-start(f32[2,4,512,256]{3,2,0,1:T(8,128)} %copy-done) | copy-start | bytes 12582916
  207.8 5.4 %copy-start.2 = (f32[2,4,512,256]{3,2,0,1:T(8,128)}, f32[2,4,512,256]{3,2,0,1:T(8,128)S(1)}, u32[]{:S(2)}) copy-start(f32[2,4,512,256]{3,2,0,1:T(8,128)S(1)} %copy.30) | copy-start | bytes 12582916
  213.1 1.3 copy-start.5
  248.6 10.1 %all-to-all-start.13 = ((f32[2,4,512,256]{3,2,1,0:T(8,128)}), f32[2,4,512,256]{3,2,1,0:T(8,128)}, u32[]{:S(2)}, u32[]{:S(2)}) async-start(f32[2,4,512,256]{3,2,1,0:T(8,128)} %broadcast_in_dim.46), calls=%async_computation.13 | async-start | bytes 8388608 | tf_op jit(solution)/shard_map/all_to_all | solution.py:13
  259.4 14.9 %all-to-all-start.11 = ((f32[32,8,128]{2,1,0:T(8,128)}), f32[32,8,128]{2,1,0:T(8,128)S(1)}, u32[]{:S(2)}, u32[]{:S(2)}) async-start(f32[32,8,128]{2,1,0:T(8,128)} %broadcast_in_dim.44), calls=%async_computation.11 | async-start | bytes 262144 | tf_op jit(solution)/shard_map/all_to_all | solution.py:13
  263.8 10.8 %copy-start.6 = (f32[4096,128]{0,1:T(8,128)S(1)}, f32[4096,128]{0,1:T(8,128)}, u32[]{:S(2)}) copy-start(f32[4096,128]{0,1:T(8,128)} %copy-done.5) | copy-start | bytes 6291460
  274.6 8.0 %copy-start.4 = (f32[2,4,512,256]{3,2,0,1:T(8,128)S(1)}, f32[2,4,512,256]{3,2,0,1:T(8,128)}, u32[]{:S(2)}) copy-start(f32[2,4,512,256]{3,2,0,1:T(8,128)} %copy.32) | copy-start | bytes 12582916
  281.3 1.3 copy-start.7
where the time goes:
time: 323 us; the launch traced here: 322 us
  blocking collectives  145 us (45%)
  waiting for transfers between devices  53.6 us (17%)
  local copies, waits for them, and re-layouts  49.4 us (15%)
  matrix products  38.5 us (12%)
  starting transfers between devices  35.1 us (11%)
    all_to_all x5, blocking collectives, copy_for_each(): return lax.all_to_all(copies, axis, split_axis=0, concat_axis=0, tiled=True)  80.7 us
    all_to_all x4, blocking collectives, summed_on_arrival(): lax.all_to_all(tiles, axis, split_axis=0, concat_axis=0, tiled=True)  64.1 us
    all_to_all x7, waiting for transfers between devices, copy_for_each(): return lax.all_to_all(copies, axis, split_axis=0, concat_axis=0, tiled=True)  53.6 us
    all_to_all x7, starting transfers between devices, copy_for_each(): return lax.all_to_all(copies, axis, split_axis=0, concat_axis=0, tiled=True)  35.1 us
    dot_general x8, matrix products, product(): jnp.dot(left, right, precision=lax.Precision.HIGHEST, preferred_element_t...  26.3 us
    broadcast_in_dim x12, local copies, waits for them, and re-layouts, copy_for_each(): copies = jnp.broadcast_to(x, (lax.axis_size(axis), *x.shape))  17.8 us
    all_to_all x5, local copies, waits for them, and re-layouts, copy_for_each(): return lax.all_to_all(copies, axis, split_axis=0, concat_axis=0, tiled=True)  16.8 us
    dot_general x4, matrix products, inner(): lax.dot_general(left, right, (((0,), (0,)), ((), ())), precision=lax.Prec...  12.2 us
  transfers between devices with their start and end apart: 7, of which 7 were waited for; matrix products, arithmetic and copies ran while one was open for 14% of the time, Pallas kernels for 0%

commit v1 on v0

v1 whole, which is shorter than its diff:
```python
import jax
import jax.numpy as jnp
from jax import lax
from jax.experimental import pallas as pl
from jax.experimental.pallas import tpu as pltpu
from jax.sharding import Mesh
from jax.sharding import PartitionSpec as P


ROW = ("y", "z")
COL = ("x", "core")
SMEM = pl.BlockSpec(memory_space=pltpu.SMEM)
VMEM = pl.BlockSpec(memory_space=pltpu.VMEM)
ANY = pl.BlockSpec(memory_space=pl.ANY)
F32, BF16 = jnp.float32, jnp.bfloat16
DISTANCES = (0, 3, 1, 2)
ROWS = 512


def dot(left, right):
    return jnp.dot(left, right, preferred_element_type=F32)


def halves(x):
    high = x.astype(BF16)
    return high, (x - high.astype(F32)).astype(BF16)


def product(left, right):
    lh, ll = halves(left)
    rh, rl = halves(right)
    wide = dot(lh, jnp.concatenate([rh, rl], axis=1))
    return wide[:, :128] + wide[:, 128:] + dot(ll, rh)


def starts(place_ref):
    out = []
    for side in range(2):
        for distance in DISTANCES:
            block = lax.rem(place_ref[0] + distance, 4) * 2 + lax.rem(place_ref[1] + side, 2)
            out.append(pl.multiple_of(block * ROWS, ROWS))
    return out


def piece_refs(refs, panel):
    own, swapped = refs[0].at[panel], refs[1].at[panel]
    moved = refs[2 + 6 * (panel % 2) : 8 + 6 * (panel % 2)]
    return [own, *moved[:3], swapped, *moved[3:]]


def fetch(pairs, sems):
    copies = [pltpu.make_async_copy(source, target, sems.at[i]) for i, (source, target) in enumerate(pairs)]
    for copy in copies:
        copy.start()
    return copies


def turned(x):
    high, low = halves(x.T)
    return jnp.concatenate([high, low], axis=0)


def project(left, values, totals, first):
    high, low = halves(values)
    wide, narrow = dot(left, high), dot(left[:128], low)
    part = wide[:128] + wide[128:] + narrow
    totals[...] = part if first else totals[...] + part


def project_kernel(place_ref, e_ref, *refs):
    pieces, (out_ref, field, held, totals, sems) = refs[:-5], refs[-5:]
    where = starts(place_ref)
    pairs = [(e_ref, field)]
    for i in range(8):
        pairs += [(piece_refs(pieces, panel)[i], held.at[panel, i]) for panel in range(2)]
    copies = fetch(pairs, sems)
    copies[0].wait()
    for i in range(8):
        left = turned(field[pl.ds(where[i], ROWS), :])
        for panel in range(2):
            copies[1 + 2 * i + panel].wait()
            project(left, held[panel, i], totals.at[panel], i == 0)
    for panel in range(2):
        out_ref[:, 8 * panel : 8 * panel + 8, :] = totals[panel].T.reshape(32, 8, 128)


def solved(place_ref, sums_ref, factors, mine, other, pair):
    gram = jnp.where(place_ref[1] == pair, mine[...], other[...])
    first = product(factors[0], sums_ref[:, 0:8, :].reshape(256, 128))
    left = sums_ref[:, 8:16, :].reshape(256, 128) - product(gram, first)
    return [halves(first), halves(product(factors[1], left))]


def moved(parts, values):
    total = None
    for (high, low), v in zip(parts, values):
        vh, vl = halves(v)
        wide = dot(vh, jnp.concatenate([high, low], axis=1))
        part = wide[:, :128] + wide[:, 128:] + dot(vl, high)
        total = part if total is None else total + part
    return total


def middle_kernel(place_ref, e_ref, sums_ref, factors_ref, mine_ref, other_ref, *refs):
    early, late = refs[:14], refs[14:26]
    out_ref, tiles_ref, field, new, sums, factors, mine, other, held, later, totals, sems, out_sems = refs[26:]
    where = starts(place_ref)
    late = (*early[:2], *late)
    pairs = [(sums_ref, sums), (factors_ref.at[0:2], factors), (mine_ref, mine), (other_ref, other), (e_ref, field)]
    for i in range(8):
        pairs += [(piece_refs(early, panel)[i], held.at[panel, i]) for panel in range(2)]
        pairs += [(piece_refs(late, 2 + panel)[i], later.at[panel, i]) for panel in range(2)]
    copies = fetch(pairs, sems)
    for copy in copies[:4]:
        copy.wait()
    parts = solved(place_ref, sums, factors, mine, other, 0)
    copies[4].wait()
    outs = []
    for i in range(8):
        rows = pl.ds(where[i], ROWS)
        for copy in copies[5 + 4 * i : 9 + 4 * i]:
            copy.wait()
        value = field[rows, :] - moved(parts, [held[0, i], held[1, i]])
        new[i] = value
        outs.append(pltpu.make_async_copy(new.at[i], out_ref.at[rows, :], out_sems.at[i]))
        outs[-1].start()
        left = turned(value)
        for panel in range(2):
            project(left, later[panel, i], totals.at[panel], i == 0)
    for panel in range(2):
        tiles_ref[:, 8 * panel : 8 * panel + 8, :] = totals[panel].T.reshape(32, 8, 128)
    for copy in outs:
        copy.wait()


def last_kernel(place_ref, field_ref, sums_ref, factors_ref, mine_ref, other_ref, *refs):
    pieces, (out_ref, field, new, sums, factors, mine, other, held, sems, out_sems) = refs[:-10], refs[-10:]
    where = starts(place_ref)
    pairs = [(sums_ref, sums), (factors_ref.at[2:4], factors), (mine_ref, mine), (other_ref, other), (field_ref, field)]
    for i in range(8):
        pairs += [(piece_refs(pieces, 2 + panel)[i], held.at[panel, i]) for panel in range(2)]
    copies = fetch(pairs, sems)
    for copy in copies[:4]:
        copy.wait()
    parts = solved(place_ref, sums, factors, mine, other, 1)
    copies[4].wait()
    outs = []
    for i in range(8):
        rows = pl.ds(where[i], ROWS)
        for copy in copies[5 + 2 * i : 7 + 2 * i]:
            copy.wait()
        new[i] = field[rows, :] - moved(parts, [held[0, i], held[1, i]])
        outs.append(pltpu.make_async_copy(new.at[i], out_ref.at[rows, :], out_sems.at[i]))
        outs[-1].start()
    for copy in outs:
        copy.wait()


def gram_kernel(place_ref, panels_ref, mine_ref, other_ref):
    for pair in range(2):
        lh, ll = halves(panels_ref[2 * pair + 1].T)
        high, low = halves(panels_ref[2 * pair])
        block = dot(lh, high) + dot(lh, low) + dot(ll, high)

        @pl.when(place_ref[1] == pair)
        def _():
            mine_ref[...] = block

        @pl.when(place_ref[1] != pair)
        def _():
            other_ref[...] = block


def spread_kernel(arrived_ref, out_ref):
    total = jnp.sum(arrived_ref[...], axis=0)
    out_ref[...] = jnp.broadcast_to(total[None], out_ref.shape)


def call(kernel, out, ins, outs, scratch, *args):
    return pl.pallas_call(kernel, out_shape=out, in_specs=ins, out_specs=outs, scratch_shapes=scratch,
                          compiler_params=pltpu.CompilerParams(vmem_limit_bytes=40 * 2**20))(*args)


def shifted(x, axis, step):
    size = lax.axis_size(axis)
    return lax.ppermute(x, axis, [(i, (i + step) % size) for i in range(size)])


def gathered(k, own):
    behind = shifted(own, "x", 1)
    ahead = shifted(own, "x", -1)
    far = shifted(*((behind, "x", 1) if k % 2 == 0 else (ahead, "x", -1)))
    mine = [behind, ahead, far]
    return mine + [shifted(part, "core", 1) for part in mine]


def exchanged(tiles):
    return lax.all_to_all(tiles, ROW, split_axis=0, concat_axis=0, tiled=True)


def total(tiles):
    arrived = exchanged(tiles)
    copies = call(spread_kernel, jax.ShapeDtypeStruct(tiles.shape, F32), [VMEM], VMEM, [], arrived)
    return exchanged(copies)


def gram(reflectors, place):
    share = jax.ShapeDtypeStruct((256, 256), F32)
    mine, other = call(gram_kernel, [share, share], [SMEM, VMEM], [VMEM, VMEM], [], place, reflectors)
    mine = mine + shifted(other, "core", 1)
    part = exchanged(mine.reshape(32, 8, 256)).sum(axis=0)
    part = (part + shifted(part, "x", 2)) + (shifted(part, "x", 1) + shifted(part, "x", -1))
    copies = jnp.broadcast_to(lax.optimization_barrier(part), (32, 8, 256))
    mine = exchanged(copies).reshape(256, 256)
    return mine, shifted(mine, "core", 1)


def body(eigvecs, reflectors, factors):
    place = jnp.stack([lax.axis_index("x"), lax.axis_index("core")]).astype(jnp.int32)
    swapped = shifted(reflectors, "core", 1)
    moving = [gathered(k, reflectors[k]) for k in range(4)]
    mine, other = gram(reflectors, place)
    whole, tiles = jax.ShapeDtypeStruct((4096, 128), F32), jax.ShapeDtypeStruct((32, 16, 128), F32)
    early, late = (*moving[0], *moving[1]), (*moving[2], *moving[3])
    sem = pltpu.SemaphoreType.DMA
    field = pltpu.VMEM((4096, 128), F32)
    held, totals = pltpu.VMEM((2, 8, ROWS, 256), F32), pltpu.VMEM((2, 128, 256), F32)
    new, square = pltpu.VMEM((8, ROWS, 128), F32), pltpu.VMEM((256, 256), F32)
    small = [pltpu.VMEM((32, 16, 128), F32), pltpu.VMEM((2, 256, 256), F32), square, square]
    sums = call(project_kernel, tiles, [SMEM] + [ANY] * 15, VMEM, [field, held, totals, sem((17,))],
                place, eigvecs, reflectors, swapped, *early)
    sums = total(sums)
    rest, sums = call(middle_kernel, [whole, tiles], [SMEM] + [ANY] * 31, [ANY, VMEM],
                      [field, new, *small, held, held, totals, sem((37,)), sem((8,))],
                      place, eigvecs, sums, factors, mine, other, reflectors, swapped, *early, *late)
    sums = total(sums)
    return call(last_kernel, whole, [SMEM] + [ANY] * 19, ANY,
                [field, new, *small, held, sem((21,)), sem((8,))],
                place, rest, sums, factors, mine, other, reflectors, swapped, *late)


def solution(mesh):
    split = Mesh(mesh.devices.reshape(4, 8, 4, 2), (*ROW, *COL))
    in_specs = (P(ROW, COL), P(None, ROW + COL, None), P())
    return jax.shard_map(body, mesh=split, in_specs=in_specs, out_specs=P(ROW, COL), check_vma=False)
```

time: 323 us -> 185 us (0.57)
  blocking collectives: 145 us -> 30.6 us
  matrix products: 38.5 us -> 0 us
  local copies, waits for them, and re-layouts: 49.4 us -> 11 us
  Pallas kernels: 0 us -> 23.8 us
  starting transfers between devices: 35.1 us -> 54.5 us
  waiting for transfers between devices: 53.6 us -> 62.9 us
    all_to_all x9 -> x2, blocking collectives: 145 us -> 30.6 us  [exchanged(): return lax.all_to_all(tiles, ROW, split_axis=0, concat_axis=0, tiled=True)]
    ppermute x0 -> x30, waiting for transfers between devices: none -> 45.7 us  [shifted(): return lax.ppermute(x, axis, [(i, (i + step) % size) for i in range(size)])]
    dot_general x12 -> x0, matrix products: 38.5 us -> none  [the longest x8 26.3 us: product(): jnp.dot(left, right, precision=lax.Precision.HIGHEST, preferred_element_t...]
    all_to_all x7 -> x4, waiting for transfers between devices: 53.6 us -> 17.2 us  [exchanged(): return lax.all_to_all(tiles, ROW, split_axis=0, concat_axis=0, tiled=True)]
    pallas_call x0 -> x6, Pallas kernels: none -> 23.8 us  [call(): pl.pallas_call(kernel, out_shape=out, in_specs=ins, out_specs=outs, scrat...]
    ppermute x0 -> x30, starting transfers between devices: none -> 19.8 us  [shifted(): return lax.ppermute(x, axis, [(i, (i + step) % size) for i in range(size)])]
    broadcast_in_dim x12 -> x1, local copies, waits for them, and re-layouts: 17.8 us -> 0.71 us  [gram(): copies = jnp.broadcast_to(lax.optimization_barrier(part), (32, 8, 256))]
    all_to_all x5 -> x0, local copies, waits for them, and re-layouts: 16.8 us -> none  [copy_for_each(): return lax.all_to_all(copies, axis, split_axis=0, concat_axis=0, tiled=True)]
  transfers between devices with their start and end apart: 7 -> 34, of which waited for: 7 -> 12; matrix products, arithmetic and copies ran while one was open for 14% -> 1% of each run, Pallas kernels for 0% -> 4%
where the time goes in v1:
time: 185 us; the launch traced here: 184 us
  waiting for transfers between devices  62.9 us (34%)
  starting transfers between devices  54.5 us (29%)
  blocking collectives  30.6 us (17%)
  Pallas kernels  23.8 us (13%)
  local copies, waits for them, and re-layouts  11 us (6%)
    ppermute x30, waiting for transfers between devices, shifted(): return lax.ppermute(x, axis, [(i, (i + step) % size) for i in range(size)])  45.7 us
    all_to_all x4, starting transfers between devices, exchanged(): return lax.all_to_all(tiles, ROW, split_axis=0, concat_axis=0, tiled=True)  34.8 us
    all_to_all x2, blocking collectives, exchanged(): return lax.all_to_all(tiles, ROW, split_axis=0, concat_axis=0, tiled=True)  30.6 us
    pallas_call x6, Pallas kernels, call(): pl.pallas_call(kernel, out_shape=out, in_specs=ins, out_specs=outs, scrat...  23.8 us
    ppermute x30, starting transfers between devices, shifted(): return lax.ppermute(x, axis, [(i, (i + step) % size) for i in range(size)])  19.8 us
    all_to_all x4, waiting for transfers between devices, exchanged(): return lax.all_to_all(tiles, ROW, split_axis=0, concat_axis=0, tiled=True)  17.2 us
    unnamed x26, local copies, waits for them, and re-layouts  9.19 us
  transfers between devices with their start and end apart: 34, of which 12 were waited for; matrix products, arithmetic and copies ran while one was open for 1% of the time, Pallas kernels for 4%

profile of v1, /device:TPU:32, one launch (start us, length us, event | category | flops | bytes accessed | tf_op | source)
XLA Modules:
  0.0 184.2 jit_solution(2615491996731099179)
XLA Ops:
  5.2 2.8 %collective-permute-start.8 = (f32[512,256]{1,0:T(8,128)S(1)}, f32[512,256]{1,0:T(8,128)S(1)}, u32[]{:S(2)}, u32[]{:S(2)}) collective-permute-start(f32[512,256]{1,0:T(8,128)S(1)} %get-tuple-element.15), channel_id=1, source_target_pairs={{0,6},{2,0},{4,2},{6,4},{1,7},{3,1},{5,3},{7,5},{8,14},{10,8},{12,... | collective-permute-start | bytes 1572872 | tf_op jit(solution)/shard_map/ppermute | solution.py:186
  7.9 3.2 %collective-permute-start.2 = (f32[512,256]{1,0:T(8,128)S(1)}, f32[512,256]{1,0:T(8,128)}, u32[]{:S(2)}, u32[]{:S(2)}) collective-permute-start(f32[512,256]{1,0:T(8,128)S(1)} %get-tuple-element.16), channel_id=1, source_target_pairs={{0,6},{2,0},{4,2},{6,4},{1,7},{3,1},{5,3},{7,5},{8,14},{10,8},{12,... | collective-permute-start | bytes 1572872 | tf_op jit(solution)/shard_map/ppermute | solution.py:186
  11.2 9.1 %collective-permute-done.8.refs_9_ = f32[512,256]{1,0:T(8,128)S(1)} collective-permute-done((f32[512,256]{1,0:T(8,128)S(1)}, f32[512,256]{1,0:T(8,128)S(1)}, u32[]{:S(2)}, u32[]{:S(2)}) %collective-permute-start.8) | collective-permute-done | bytes 524320 | tf_op jit(solution)/shard_map/ppermute | solution.py:186
  20.2 3.7 %collective-permute-done.7.refs_8_ = f32[512,256]{1,0:T(8,128)S(1)} collective-permute-done((f32[512,256]{1,0:T(8,128)S(1)}, f32[512,256]{1,0:T(8,128)S(1)}, u32[]{:S(2)}, u32[]{:S(2)}) %collective-permute-start.7) | collective-permute-done | bytes 524320 | tf_op jit(solution)/shard_map/ppermute | solution.py:186
  23.9 7.5 %collective-permute-done.2.refs_3_ = f32[512,256]{1,0:T(8,128)} collective-permute-done((f32[512,256]{1,0:T(8,128)S(1)}, f32[512,256]{1,0:T(8,128)}, u32[]{:S(2)}, u32[]{:S(2)}) %collective-permute-start.2) | collective-permute-done | bytes 524320 | tf_op jit(solution)/shard_map/ppermute | solution.py:186
  31.5 2.6 %collective-permute-done.1.refs_2_ = f32[512,256]{1,0:T(8,128)} collective-permute-done((f32[512,256]{1,0:T(8,128)S(1)}, f32[512,256]{1,0:T(8,128)}, u32[]{:S(2)}, u32[]{:S(2)}) %collective-permute-start.1) | collective-permute-done | bytes 524320 | tf_op jit(solution)/shard_map/ppermute | solution.py:186
  34.9 6.9 %collective-permute-done.9.refs_10_ = f32[512,256]{1,0:T(8,128)} collective-permute-done((f32[512,256]{1,0:T(8,128)S(1)}, f32[512,256]{1,0:T(8,128)}, u32[]{:S(2)}, u32[]{:S(2)}) %collective-permute-start.9) | collective-permute-done | bytes 524320 | tf_op jit(solution)/shard_map/ppermute | solution.py:186
  43.1 5.2 %collective-permute-done.3.refs_4_ = f32[512,256]{1,0:T(8,128)} collective-permute-done((f32[512,256]{1,0:T(8,128)}, f32[512,256]{1,0:T(8,128)}, u32[]{:S(2)}, u32[]{:S(2)}) %collective-permute-start.3) | collective-permute-done | bytes 524320 | tf_op jit(solution)/shard_map/ppermute | solution.py:186
  49.0 11.4 %all-to-all-start.2 = ((f32[32,8,256]{2,1,0:T(8,128)}), f32[32,8,256]{2,1,0:T(8,128)S(1)}, u32[]{:S(2)}, u32[]{:S(2)}) async-start(f32[32,8,256]{2,1,0:T(8,128)} %add_bitcast_fusion), calls=%async_computation.2 | async-start | bytes 524288 | tf_op jit(solution)/shard_map/all_to_all | solution.py:198
  60.4 1.7 collective-permute-start.25
  66.2 6.3 %shard_map.37 = f32[32,16,128]{2,1,0:T(8,128)} custom-call(s32[2]{0:T(128)S(1)} %pad_add_fusion.place_ref, f32[4096,128]{1,0:T(8,128)S(1)} %copy-done.3, f32[4,512,256]{2,1,0:T(8,128)S(1)} %copy-done.1, f32[4,512,256]{2,1,0:T(8,128)} %collective-permute-done.refs_1_, f32[512,256]{1,0:T(8,128)} %collective-permute-done.1.refs_2_, ...), custom_call_target="tpu_custom_call" | custom-call | tf_op jit(solution)/shard_map/pallas_call | solution.py:180
  73.3 9.2 %all-to-all-start = ((f32[32,16,128]{2,1,0:T(8,128)}), f32[32,16,128]{2,1,0:T(8,128)S(1)}, u32[]{:S(2)}, u32[]{:S(2)}) async-start(f32[32,16,128]{2,1,0:T(8,128)} %shard_map.37), calls=%async_computation | async-start | bytes 524288 | tf_op jit(solution)/shard_map/all_to_all | solution.py:198
  82.6 3.3 %collective-permute-start.16 = (f32[8,256]{1,0:T(8,128)S(1)}, f32[8,256]{1,0:T(8,128)S(1)}, u32[]{:S(2)}, u32[]{:S(2)}) collective-permute-start(f32[8,256]{1,0:T(8,128)S(1)} %reduce_sum.9), channel_id=1, source_target_pairs={{0,6},{2,0},{4,2},{6,4},{1,7},{3,1},{5,3},{7,5},{8,14},{10,8},{12,... | collective-permute-start | bytes 24584 | tf_op jit(solution)/shard_map/ppermute | solution.py:186
  85.9 3.1 %collective-permute-start.14 = (f32[8,256]{1,0:T(8,128)S(1)}, f32[8,256]{1,0:T(8,128)S(1)}, u32[]{:S(2)}, u32[]{:S(2)}) collective-permute-start(f32[8,256]{1,0:T(8,128)S(1)} %reduce_sum.9), channel_id=1, source_target_pairs={{0,4},{2,6},{4,0},{6,2},{1,5},{3,7},{5,1},{7,3},{8,12},{10,14},{12... | collective-permute-start | bytes 24584 | tf_op jit(solution)/shard_map/ppermute | solution.py:186
  89.7 7.1 %collective-permute-done.15 = f32[8,256]{1,0:T(8,128)S(1)} collective-permute-done((f32[8,256]{1,0:T(8,128)S(1)}, f32[8,256]{1,0:T(8,128)S(1)}, u32[]{:S(2)}, u32[]{:S(2)}) %collective-permute-start.15) | collective-permute-done | bytes 8224 | tf_op jit(solution)/shard_map/ppermute | solution.py:186
  99.6 9.8 %all-to-all-start.3 = ((f32[32,8,256]{2,1,0:T(8,128)}), f32[32,8,256]{2,1,0:T(8,128)S(1)}, u32[]{:S(2)}, u32[]{:S(2)}) async-start(f32[32,8,256]{2,1,0:T(8,128)} %broadcast_in_dim.3), calls=%async_computation.3 | async-start | bytes 524288 | tf_op jit(solution)/shard_map/all_to_all | solution.py:198
  110.2 2.1 %collective-permute-done.26.refs_22_.refs_10_ = f32[512,256]{1,0:T(8,128)} collective-permute-done((f32[512,256]{1,0:T(8,128)}, f32[512,256]{1,0:T(8,128)}, u32[]{:S(2)}, u32[]{:S(2)}) %collective-permute-start.26) | collective-permute-done | bytes 524320 | tf_op jit(solution)/shard_map/ppermute | solution.py:186
  113.5 6.9 %all-to-all-done.3 = f32[32,8,256]{2,1,0:T(8,128)S(1)} async-done(((f32[32,8,256]{2,1,0:T(8,128)}), f32[32,8,256]{2,1,0:T(8,128)S(1)}, u32[]{:S(2)}, u32[]{:S(2)}) %all-to-all-start.3) | async-done | bytes 262176 | tf_op jit(solution)/shard_map/all_to_all | solution.py:198
  120.4 4.5 %all-to-all-start.1 = ((f32[32,16,128]{2,1,0:T(8,128)}), f32[32,16,128]{2,1,0:T(8,128)S(1)}, u32[]{:S(2)}, u32[]{:S(2)}) async-start(f32[32,16,128]{2,1,0:T(8,128)} %copy-done.12), calls=%async_computation.1 | async-start | bytes 524288 | tf_op jit(solution)/shard_map/all_to_all | solution.py:198
  126.5 9.5 %all-to-all-done.1.sums_ref = f32[32,16,128]{2,1,0:T(8,128)S(1)} async-done(((f32[32,16,128]{2,1,0:T(8,128)}), f32[32,16,128]{2,1,0:T(8,128)S(1)}, u32[]{:S(2)}, u32[]{:S(2)}) %all-to-all-start.1) | async-done | bytes 262176 | tf_op jit(solution)/shard_map/all_to_all | solution.py:198
  136.0 9.5 %shard_map.40 = (f32[4096,128]{1,0:T(8,128)}, f32[32,16,128]{2,1,0:T(8,128)S(1)}) custom-call(s32[2]{0:T(128)S(1)} %pad_add_fusion.place_ref, f32[4096,128]{1,0:T(8,128)} %e_ref.3, f32[32,16,128]{2,1,0:T(8,128)S(1)} %all-to-all-done.1.sums_ref, f32[4,256,256]{2,1,0:T(8,128)} %factors_ref.3, f32[256,256]{1,0:T(8,128)S(1)} %bitcast.14, ...), custom_call_target="tpu_custom_call" | custom-call | tf_op jit(solution)/shard_map/pallas_call | solution.py:180
  145.6 15.3 %all_to_all.30.arrived_ref = f32[32,16,128]{2,1,0:T(8,128)S(1)} all-to-all(f32[32,16,128]{2,1,0:T(8,128)S(1)} %get-tuple-element.12), channel_id=1, replica_groups=mesh['y'=4,'z'=8,'x'=4,'core'=2] {'y','z'}, dimensions={0} | all-to-all | bytes 524288 | tf_op jit(solution)/shard_map/all_to_all | solution.py:198
  160.9 15.3 %all_to_all.31.sums_ref = f32[32,16,128]{2,1,0:T(8,128)S(1)} all-to-all(f32[32,16,128]{2,1,0:T(8,128)S(1)} %shard_map.41), channel_id=1, replica_groups=mesh['y'=4,'z'=8,'x'=4,'core'=2] {'y','z'}, dimensions={0} | all-to-all | bytes 524288 | tf_op jit(solution)/shard_map/all_to_all | solution.py:198
  177.8 6.2 %shard_map.42 = f32[4096,128]{1,0:T(8,128)} custom-call(s32[2]{0:T(128)S(1)} %pad_add_fusion.place_ref, f32[4096,128]{1,0:T(8,128)S(1)} %copy-done.5, f32[32,16,128]{2,1,0:T(8,128)S(1)} %all_to_all.31.sums_ref, f32[4,256,256]{2,1,0:T(8,128)S(1)} %copy-done.4, f32[256,256]{1,0:T(8,128)S(1)} %bitcast.15, f32[256,256]{1,0:T(8,128)S(1)} %collective-permute-done.17.other_ref, ...), custom_call_target="tpu_custom_call" | custom-call | tf_op jit(solution)/shard_map/pallas_call | solution.py:180
  (84 shorter events, 21.7 us)
Async XLA Ops:
  0.0 62.5 %collective-permute-start = (f32[4,512,256]{2,1,0:T(8,128)}, f32[4,512,256]{2,1,0:T(8,128)}, u32[]{:S(2)}, u32[]{:S(2)}) collective-permute-start(f32[4,512,256]{2,1,0:T(8,128)} %refs_0_.5), channel_id=1, source_target_pairs={{0,1},{1,0},{2,3},{3,2},{4,5},{5,4},{6,7},{7,6},{8,9},{9,8},{10,11... | collective-permute-start | bytes 6291464 | tf_op jit(solution)/shard_map/ppermute | solution.py:186
  5.2 15.1 %collective-permute-start.8 = (f32[512,256]{1,0:T(8,128)S(1)}, f32[512,256]{1,0:T(8,128)S(1)}, u32[]{:S(2)}, u32[]{:S(2)}) collective-permute-start(f32[512,256]{1,0:T(8,128)S(1)} %get-tuple-element.15), channel_id=1, source_target_pairs={{0,6},{2,0},{4,2},{6,4},{1,7},{3,1},{5,3},{7,5},{8,14},{10,8},{12,... | collective-permute-start | bytes 1572872 | tf_op jit(solution)/shard_map/ppermute | solution.py:186
  7.9 16.0 %collective-permute-start.7 = (f32[512,256]{1,0:T(8,128)S(1)}, f32[512,256]{1,0:T(8,128)S(1)}, u32[]{:S(2)}, u32[]{:S(2)}) collective-permute-start(f32[512,256]{1,0:T(8,128)S(1)} %get-tuple-element.15), channel_id=1, source_target_pairs={{0,2},{2,4},{4,6},{6,0},{1,3},{3,5},{5,7},{7,1},{8,10},{10,12},{12... | collective-permute-start | bytes 1572872 | tf_op jit(solution)/shard_map/ppermute | solution.py:186
  7.9 23.5 %collective-permute-start.2 = (f32[512,256]{1,0:T(8,128)S(1)}, f32[512,256]{1,0:T(8,128)}, u32[]{:S(2)}, u32[]{:S(2)}) collective-permute-start(f32[512,256]{1,0:T(8,128)S(1)} %get-tuple-element.16), channel_id=1, source_target_pairs={{0,6},{2,0},{4,2},{6,4},{1,7},{3,1},{5,3},{7,5},{8,14},{10,8},{12,... | collective-permute-start | bytes 1572872 | tf_op jit(solution)/shard_map/ppermute | solution.py:186
  11.2 22.9 %collective-permute-start.1 = (f32[512,256]{1,0:T(8,128)S(1)}, f32[512,256]{1,0:T(8,128)}, u32[]{:S(2)}, u32[]{:S(2)}) collective-permute-start(f32[512,256]{1,0:T(8,128)S(1)} %get-tuple-element.16), channel_id=1, source_target_pairs={{0,2},{2,4},{4,6},{6,0},{1,3},{3,5},{5,7},{7,1},{8,10},{10,12},{12... | collective-permute-start | bytes 1572872 | tf_op jit(solution)/shard_map/ppermute | solution.py:186
  23.9 17.8 %collective-permute-start.9 = (f32[512,256]{1,0:T(8,128)S(1)}, f32[512,256]{1,0:T(8,128)}, u32[]{:S(2)}, u32[]{:S(2)}) collective-permute-start(f32[512,256]{1,0:T(8,128)S(1)} %collective-permute-done.8.refs_9_), channel_id=1, source_target_pairs={{0,6},{2,0},{4,2},{6,4},{1,7},{3,1},{5,3},{7,5},{8,14},{10,8},{12,... | collective-permute-start | bytes 1572872 | tf_op jit(solution)/shard_map/ppermute | solution.py:186
  34.9 25.5 %collective-permute-start.5 = (f32[512,256]{1,0:T(8,128)}, f32[512,256]{1,0:T(8,128)}, u32[]{:S(2)}, u32[]{:S(2)}) collective-permute-start(f32[512,256]{1,0:T(8,128)} %collective-permute-done.2.refs_3_), channel_id=1, source_target_pairs={{0,1},{1,0},{2,3},{3,2},{4,5},{5,4},{6,7},{7,6},{8,9},{9,8},{10,11... | collective-permute-start | bytes 1572872 | tf_op jit(solution)/shard_map/ppermute | solution.py:186
  41.8 20.4 %collective-permute-start.4 = (f32[512,256]{1,0:T(8,128)}, f32[512,256]{1,0:T(8,128)}, u32[]{:S(2)}, u32[]{:S(2)}) collective-permute-start(f32[512,256]{1,0:T(8,128)} %collective-permute-done.1.refs_2_), channel_id=1, source_target_pairs={{0,1},{1,0},{2,3},{3,2},{4,5},{5,4},{6,7},{7,6},{8,9},{9,8},{10,11... | collective-permute-start | bytes 1572872 | tf_op jit(solution)/shard_map/ppermute | solution.py:186
  42.6 19.9 %collective-permute-start.12 = (f32[512,256]{1,0:T(8,128)}, f32[512,256]{1,0:T(8,128)}, u32[]{:S(2)}, u32[]{:S(2)}) collective-permute-start(f32[512,256]{1,0:T(8,128)} %collective-permute-done.9.refs_10_), channel_id=1, source_target_pairs={{0,1},{1,0},{2,3},{3,2},{4,5},{5,4},{6,7},{7,6},{8,9},{9,8},{10,11... | collective-permute-start | bytes 1572872 | tf_op jit(solution)/shard_map/ppermute | solution.py:186
  49.0 24.3 %all-to-all-start.2 = ((f32[32,8,256]{2,1,0:T(8,128)}), f32[32,8,256]{2,1,0:T(8,128)S(1)}, u32[]{:S(2)}, u32[]{:S(2)}) async-start(f32[32,8,256]{2,1,0:T(8,128)} %add_bitcast_fusion), calls=%async_computation.2 | async-start | bytes 524288 | tf_op jit(solution)/shard_map/all_to_all | solution.py:198
  60.4 25.5 %collective-permute-start.25 = (f32[512,256]{1,0:T(8,128)}, f32[512,256]{1,0:T(8,128)}, u32[]{:S(2)}, u32[]{:S(2)}) collective-permute-start(f32[512,256]{1,0:T(8,128)} %get-tuple-element.13), channel_id=1, source_target_pairs={{0,6},{2,0},{4,2},{6,4},{1,7},{3,1},{5,3},{7,5},{8,14},{10,8},{12,... | collective-permute-start | bytes 1572872 | tf_op jit(solution)/shard_map/ppermute | solution.py:186
  62.1 26.9 %collective-permute-start.18 = (f32[512,256]{1,0:T(8,128)}, f32[512,256]{1,0:T(8,128)}, u32[]{:S(2)}, u32[]{:S(2)}) collective-permute-start(f32[512,256]{1,0:T(8,128)} %get-tuple-element.14), channel_id=1, source_target_pairs={{0,2},{2,4},{4,6},{6,0},{1,3},{3,5},{5,7},{7,1},{8,10},{10,12},{12... | collective-permute-start | bytes 1572872 | tf_op jit(solution)/shard_map/ppermute | solution.py:186
  73.3 25.6 %all-to-all-start = ((f32[32,16,128]{2,1,0:T(8,128)}), f32[32,16,128]{2,1,0:T(8,128)S(1)}, u32[]{:S(2)}, u32[]{:S(2)}) async-start(f32[32,16,128]{2,1,0:T(8,128)} %shard_map.37), calls=%async_computation | async-start | bytes 524288 | tf_op jit(solution)/shard_map/all_to_all | solution.py:198
  82.5 27.0 %collective-permute-start.24 = (f32[512,256]{1,0:T(8,128)}, f32[512,256]{1,0:T(8,128)S(1)}, u32[]{:S(2)}, u32[]{:S(2)}) collective-permute-start(f32[512,256]{1,0:T(8,128)} %get-tuple-element.13), channel_id=1, source_target_pairs={{0,2},{2,4},{4,6},{6,0},{1,3},{3,5},{5,7},{7,1},{8,10},{10,12},{12... | collective-permute-start | bytes 1572872 | tf_op jit(solution)/shard_map/ppermute | solution.py:186
  89.0 20.5 %collective-permute-start.19 = (f32[512,256]{1,0:T(8,128)}, f32[512,256]{1,0:T(8,128)}, u32[]{:S(2)}, u32[]{:S(2)}) collective-permute-start(f32[512,256]{1,0:T(8,128)} %get-tuple-element.14), channel_id=1, source_target_pairs={{0,6},{2,0},{4,2},{6,4},{1,7},{3,1},{5,3},{7,5},{8,14},{10,8},{12,... | collective-permute-start | bytes 1572872 | tf_op jit(solution)/shard_map/ppermute | solution.py:186
  89.7 20.3 %collective-permute-start.28 = (f32[512,256]{1,0:T(8,128)}, f32[512,256]{1,0:T(8,128)}, u32[]{:S(2)}, u32[]{:S(2)}) collective-permute-start(f32[512,256]{1,0:T(8,128)} %collective-permute-done.25.refs_21_.refs_9_), channel_id=1, source_target_pairs={{0,1},{1,0},{2,3},{3,2},{4,5},{5,4},{6,7},{7,6},{8,9},{9,8},{10,11... | collective-permute-start | bytes 1572872 | tf_op jit(solution)/shard_map/ppermute | solution.py:186
  96.9 15.3 %collective-permute-start.26 = (f32[512,256]{1,0:T(8,128)}, f32[512,256]{1,0:T(8,128)}, u32[]{:S(2)}, u32[]{:S(2)}) collective-permute-start(f32[512,256]{1,0:T(8,128)} %collective-permute-done.25.refs_21_.refs_9_), channel_id=1, source_target_pairs={{0,6},{2,0},{4,2},{6,4},{1,7},{3,1},{5,3},{7,5},{8,14},{10,8},{12,... | collective-permute-start | bytes 1572872 | tf_op jit(solution)/shard_map/ppermute | solution.py:186
  99.6 20.8 %all-to-all-start.3 = ((f32[32,8,256]{2,1,0:T(8,128)}), f32[32,8,256]{2,1,0:T(8,128)S(1)}, u32[]{:S(2)}, u32[]{:S(2)}) async-start(f32[32,8,256]{2,1,0:T(8,128)} %broadcast_in_dim.3), calls=%async_computation.3 | async-start | bytes 524288 | tf_op jit(solution)/shard_map/all_to_all | solution.py:198
  109.4 15.5 %collective-permute-start.27 = (f32[512,256]{1,0:T(8,128)S(1)}, f32[512,256]{1,0:T(8,128)}, u32[]{:S(2)}, u32[]{:S(2)}) collective-permute-start(f32[512,256]{1,0:T(8,128)S(1)} %collective-permute-done.24.refs_20_.refs_8_), channel_id=1, source_target_pairs={{0,1},{1,0},{2,3},{3,2},{4,5},{5,4},{6,7},{7,6},{8,9},{9,8},{10,11... | collective-permute-start | bytes 1572872 | tf_op jit(solution)/shard_map/ppermute | solution.py:186
  109.6 15.5 %collective-permute-start.21 = (f32[512,256]{1,0:T(8,128)}, f32[512,256]{1,0:T(8,128)}, u32[]{:S(2)}, u32[]{:S(2)}) collective-permute-start(f32[512,256]{1,0:T(8,128)} %collective-permute-done.18.refs_14_.refs_2_), channel_id=1, source_target_pairs={{0,1},{1,0},{2,3},{3,2},{4,5},{5,4},{6,7},{7,6},{8,9},{9,8},{10,11... | collective-permute-start | bytes 1572872 | tf_op jit(solution)/shard_map/ppermute | solution.py:186
  110.1 15.0 %collective-permute-start.22 = (f32[512,256]{1,0:T(8,128)}, f32[512,256]{1,0:T(8,128)}, u32[]{:S(2)}, u32[]{:S(2)}) collective-permute-start(f32[512,256]{1,0:T(8,128)} %collective-permute-done.19.refs_15_.refs_3_), channel_id=1, source_target_pairs={{0,1},{1,0},{2,3},{3,2},{4,5},{5,4},{6,7},{7,6},{8,9},{9,8},{10,11... | collective-permute-start | bytes 1572872 | tf_op jit(solution)/shard_map/ppermute | solution.py:186
  112.2 14.3 %collective-permute-start.29 = (f32[512,256]{1,0:T(8,128)}, f32[512,256]{1,0:T(8,128)}, u32[]{:S(2)}, u32[]{:S(2)}) collective-permute-start(f32[512,256]{1,0:T(8,128)} %collective-permute-done.26.refs_22_.refs_10_), channel_id=1, source_target_pairs={{0,1},{1,0},{2,3},{3,2},{4,5},{5,4},{6,7},{7,6},{8,9},{9,8},{10,11... | collective-permute-start | bytes 1572872 | tf_op jit(solution)/shard_map/ppermute | solution.py:186
  112.2 14.3 %collective-permute-start.23 = (f32[512,256]{1,0:T(8,128)}, f32[512,256]{1,0:T(8,128)}, u32[]{:S(2)}, u32[]{:S(2)}) collective-permute-start(f32[512,256]{1,0:T(8,128)} %collective-permute-done.20.refs_16_.refs_4_), channel_id=1, source_target_pairs={{0,1},{1,0},{2,3},{3,2},{4,5},{5,4},{6,7},{7,6},{8,9},{9,8},{10,11... | collective-permute-start | bytes 1572872 | tf_op jit(solution)/shard_map/ppermute | solution.py:186
  120.4 15.6 %all-to-all-start.1 = ((f32[32,16,128]{2,1,0:T(8,128)}), f32[32,16,128]{2,1,0:T(8,128)S(1)}, u32[]{:S(2)}, u32[]{:S(2)}) async-start(f32[32,16,128]{2,1,0:T(8,128)} %copy-done.12), calls=%async_computation.1 | async-start | bytes 524288 | tf_op jit(solution)/shard_map/all_to_all | solution.py:198
  (23 other events, 372.4 us)

commit v2 on v1

v2 whole, which is shorter than its diff:
```python
import functools

import jax
import jax.numpy as jnp
from jax import lax
from jax.experimental import pallas as pl
from jax.experimental.pallas import tpu as pltpu
from jax.sharding import Mesh
from jax.sharding import PartitionSpec as P


ROW = ("y", "z")
COL = ("x", "core")
SMEM = pl.BlockSpec(memory_space=pltpu.SMEM)
VMEM = pl.BlockSpec(memory_space=pltpu.VMEM)
ANY = pl.BlockSpec(memory_space=pltpu.HBM)
F32, BF16 = jnp.float32, jnp.bfloat16
DISTANCES = (0, 3, 1, 2)
ROWS = 512
BLOCKS = ((1, 0), (2, 0), (2, 1), (3, 0), (3, 1), (3, 2))


def dot(left, right):
    return jnp.dot(left, right, preferred_element_type=F32)


def halves(x):
    high = x.astype(BF16)
    return high, (x - high.astype(F32)).astype(BF16)


def product(left, right):
    lh, ll = halves(left)
    rh, rl = halves(right)
    wide = dot(lh, jnp.concatenate([rh, rl], axis=1))
    return wide[:, :128] + wide[:, 128:] + dot(ll, rh)


def starts(place_ref):
    out = []
    for side in range(2):
        for distance in DISTANCES:
            block = lax.rem(place_ref[0] + distance, 4) * 2 + lax.rem(place_ref[1] + side, 2)
            out.append(pl.multiple_of(block * ROWS, ROWS))
    return out


def fetch(pairs, sems):
    copies = [pltpu.make_async_copy(source, target, sems.at[i]) for i, (source, target) in enumerate(pairs)]
    for copy in copies:
        copy.start()
    return copies


def panel_of(piece, panel):
    return piece.at[panel if piece.shape[0] == 4 else panel % 2]


def turned(x):
    high, low = halves(x.T)
    return jnp.concatenate([high, low], axis=0)


def crossed(left, high, low):
    wide = dot(left, high)
    return wide[:128] + wide[128:] + dot(left[:128], low)


def stage_kernel(items, first, last, place_ref, e_ref, *refs):
    olds, refs = (refs[:0], refs) if first else (refs[:1], refs[1:])
    pieces, (out_ref, field, held, sums, sems) = refs[: len(items)], refs[len(items) :]
    where = starts(place_ref)
    blocks = sorted({block for block, _ in items})
    pairs, need = [], {}
    for at, block in enumerate(blocks):
        need[block] = len(pairs)
        pairs.append((e_ref.at[pl.ds(where[block], ROWS), :], field.at[at]))
        for i, (its_block, pair) in enumerate(items):
            if its_block == block:
                for k in range(2):
                    need[i, k] = len(pairs)
                    pairs.append((panel_of(pieces[i], 2 * pair + k), held.at[2 * i + k]))
    pairs += list(zip(olds, [sums]))
    copies = fetch(pairs, sems)
    if first:
        sums[...] = jnp.zeros_like(sums)
    else:
        copies[-1].wait()
    for at, block in enumerate(blocks):
        copies[need[block]].wait()
        left = turned(field[at])
        for i, (its_block, pair) in enumerate(items):
            if its_block == block:
                for k in range(2):
                    copies[need[i, k]].wait()
                    sums[2 * pair + k] += crossed(left, *halves(held[2 * i + k]))
    if last:
        for k in range(4):
            out_ref[:, 8 * k : 8 * k + 8, :] = sums[k].T.reshape(32, 8, 128)
    else:
        end = pltpu.make_async_copy(sums, out_ref, sems.at[0])
        end.start()
        end.wait()


def hold_kernel(*refs):
    pieces, (out_ref, held, split, sems, out_sems) = refs[:16], refs[16:]
    slots = held.shape[0]

    def copies(block):
        slot = block % slots
        return [pltpu.make_async_copy(panel_of(pieces[2 * block + k // 2], k), held.at[slot, k], sems.at[slot, k]) for k in range(4)]

    def out(block):
        return pltpu.make_async_copy(split.at[block % 2], out_ref.at[block], out_sems.at[block % 2])

    for block in range(slots - 1):
        for copy in copies(block):
            copy.start()
    for block in range(8):
        if block + slots - 1 < 8:
            for copy in copies(block + slots - 1):
                copy.start()
        if block >= 2:
            out(block - 2).wait()
        for k, copy in enumerate(copies(block)):
            copy.wait()
            split[block % 2, k, 0], split[block % 2, k, 1] = halves(held[block % slots, k])
        out(block).start()
    out(6).wait()
    out(7).wait()


def last_kernel(place_ref, field_ref, factors_ref, sums_ref, mine_ref, other_ref, held_ref, out_ref,
                field, new, factors, sums, mine, other, held, sems, out_sems):
    where = starts(place_ref)
    pairs = [(sums_ref, sums), (factors_ref, factors), (mine_ref, mine), (other_ref, other)]
    for block in range(8):
        pairs += [(field_ref.at[pl.ds(where[block], ROWS), :], field.at[block]), (held_ref.at[block], held.at[block])]
    copies = fetch(pairs, sems)
    for copy in copies[:4]:
        copy.wait()

    def gram(k, j):
        half, at = divmod(BLOCKS.index((k, j)), 3)
        rows = pl.ds(256 * at, 256)
        return jnp.where(place_ref[1] == half, mine[rows, :], other[rows, :])

    coeffs = []
    for k in range(4):
        left = sums[:, 8 * k : 8 * k + 8, :].reshape(256, 128)
        for j in range(k):
            left = left - product(gram(k, j), coeffs[j])
        coeffs.append(product(factors[k], left))
    parts = []
    for high, low in map(halves, coeffs):
        parts.append((jnp.concatenate([high, low], axis=1), high))
    outs = []
    for block in range(8):
        copies[4 + 2 * block].wait()
        copies[5 + 2 * block].wait()
        total = None
        for k, (wide, high) in enumerate(parts):
            both = dot(held[block, k, 0], wide)
            part = both[:, :128] + both[:, 128:] + dot(held[block, k, 1], high)
            total = part if total is None else total + part
        new[block] = field[block] - total
        outs.append(pltpu.make_async_copy(new.at[block], out_ref.at[pl.ds(where[block], ROWS), :], out_sems.at[block]))
        outs[-1].start()
    for copy in outs:
        copy.wait()


def gram_kernel(place_ref, first_ref, second_ref, mine_ref, other_ref):
    panels = [first_ref[0], first_ref[1], second_ref[0], second_ref[1]]
    parts = [halves(panel) for panel in panels[:3]]
    for k in range(1, 4):
        lh, ll = halves(panels[k].T)
        for j in range(k):
            high, low = parts[j]
            block = dot(lh, high) + dot(lh, low) + dot(ll, high)
            half, at = divmod(BLOCKS.index((k, j)), 3)

            @pl.when(place_ref[1] == half)
            def _():
                mine_ref[256 * at : 256 * at + 256, :] = block

            @pl.when(place_ref[1] != half)
            def _():
                other_ref[256 * at : 256 * at + 256, :] = block


def spread_kernel(arrived_ref, out_ref):
    total = jnp.sum(arrived_ref[...], axis=0)
    out_ref[...] = jnp.broadcast_to(total[None], out_ref.shape)


def call(kernel, out, ins, outs, scratch, *args, limit=None):
    limit = limit or (60 if scratch else 16)
    return pl.pallas_call(kernel, out_shape=out, in_specs=ins, out_specs=outs, scratch_shapes=scratch,
                          compiler_params=pltpu.CompilerParams(vmem_limit_bytes=limit * 2**20))(*args)


def shifted(x, axis, step):
    size = lax.axis_size(axis)
    return lax.ppermute(x, axis, [(i, (i + step) % size) for i in range(size)])


def gathered(pair, own):
    behind = shifted(own, "x", 1)
    ahead = shifted(own, "x", -1)
    far = shifted(*((behind, "x", 1) if pair == 0 else (ahead, "x", -1)))
    mine = [behind, ahead, far]
    swapped = [shifted(part, "core", 1) for part in mine]
    return dict(zip((1, 2, 3, 5, 6, 7), mine + swapped))


def exchanged(tiles):
    return lax.all_to_all(tiles, ROW, split_axis=0, concat_axis=0, tiled=True)


def total(tiles):
    arrived = exchanged(tiles)
    copies = call(spread_kernel, jax.ShapeDtypeStruct(tiles.shape, F32), [VMEM], VMEM, [], arrived)
    return exchanged(copies)


def gram(pairs, place):
    share = jax.ShapeDtypeStruct((768, 256), F32)
    mine, other = call(gram_kernel, [share, share], [SMEM, VMEM, VMEM], [VMEM, VMEM], [], place, *pairs)
    mine = mine + shifted(other, "core", 1)
    part = exchanged(mine.reshape(32, 24, 256)).sum(axis=0)
    part = (part + shifted(part, "x", 2)) + (shifted(part, "x", 1) + shifted(part, "x", -1))
    copies = jnp.broadcast_to(lax.optimization_barrier(part), (32, 24, 256))
    mine = exchanged(copies).reshape(768, 256)
    return mine, shifted(mine, "core", 1)


def body(eigvecs, reflectors, factors):
    place = jnp.stack([lax.axis_index("x"), lax.axis_index("core")]).astype(jnp.int32)
    sem = pltpu.SemaphoreType.DMA
    own = [reflectors[:2], reflectors[2:]]
    swapped = shifted(reflectors, "core", 1)
    moving = [gathered(pair, own[pair]) for pair in range(2)]
    mine, other = gram(own, place)
    piece = lambda block, pair: {0: reflectors, 4: swapped}.get(block, moving[pair].get(block))
    everything = [piece(block, pair) for block in range(8) for pair in range(2)]

    def stage(items, olds, out, last=False):
        count = len({block for block, _ in items})
        return call(functools.partial(stage_kernel, items, not olds, last), out,
                    [SMEM, ANY] + [ANY] * (len(olds) + len(items)), VMEM if last else ANY,
                    [pltpu.VMEM((count, ROWS, 128), F32), pltpu.VMEM((2 * len(items), ROWS, 256), F32),
                     pltpu.VMEM((4, 128, 256), F32), sem((count + 2 * len(items) + 1,))],
                    place, eigvecs, *olds, *[piece(*item) for item in items])

    sums, tiles = jax.ShapeDtypeStruct((4, 128, 256), F32), jax.ShapeDtypeStruct((32, 32, 128), F32)
    state = stage(((0, 0), (0, 1), (4, 0), (4, 1)), [], sums)
    state = stage(((1, 0), (2, 1), (5, 0), (6, 1)), [state], sums)
    state = stage(((1, 1), (2, 0), (5, 1), (6, 0)), [state], sums)
    sums = total(stage(((3, 0), (3, 1), (7, 0), (7, 1)), [state], tiles, last=True))
    held = jax.ShapeDtypeStruct((8, 4, 2, ROWS, 256), BF16)
    held = call(hold_kernel, held, [ANY] * 16, ANY,
                [pltpu.VMEM((3, 4, ROWS, 256), F32), pltpu.VMEM((2, 4, 2, ROWS, 256), BF16), sem((3, 4)), sem((2,))], *everything)
    block = pltpu.VMEM((8, ROWS, 128), F32)
    share = pltpu.VMEM((768, 256), F32)
    return call(last_kernel, jax.ShapeDtypeStruct((4096, 128), F32), [SMEM] + [ANY] * 6, ANY,
                [block, block, pltpu.VMEM((4, 256, 256), F32), pltpu.VMEM((32, 32, 128), F32), share, share,
                 pltpu.VMEM((8, 4, 2, ROWS, 256), BF16), sem((20,)), sem((8,))],
                place, eigvecs, factors, sums, mine, other, held)


def solution(mesh):
    split = Mesh(mesh.devices.reshape(4, 8, 4, 2), (*ROW, *COL))
    in_specs = (P(ROW, COL), P(None, ROW + COL, None), P())
    return jax.shard_map(body, mesh=split, in_specs=in_specs, out_specs=P(ROW, COL), check_vma=False)
```

time: 185 us -> 198 us (1.070)
  blocking collectives: 30.6 us -> 0 us
  Pallas kernels: 23.8 us -> 53.9 us
  waiting for transfers between devices: 62.9 us -> 89.4 us
  starting transfers between devices: 54.5 us -> 46.5 us
  local copies, waits for them, and re-layouts: 11 us -> 4.46 us
    all_to_all x2 -> x0, blocking collectives: 30.6 us -> none  [exchanged(): return lax.all_to_all(tiles, ROW, split_axis=0, concat_axis=0, tiled=True)]
    pallas_call x6 -> x8, Pallas kernels: 23.8 us -> 53.9 us  [call(): pl.pallas_call(kernel, out_shape=out, in_specs=ins, out_specs=outs, scrat...]
    all_to_all x4, waiting for transfers between devices: 17.2 us -> 35.2 us  [exchanged(): return lax.all_to_all(tiles, ROW, split_axis=0, concat_axis=0, tiled=True)]
    ppermute x30 -> x18, waiting for transfers between devices: 45.7 us -> 54.2 us  [shifted(): return lax.ppermute(x, axis, [(i, (i + step) % size) for i in range(size)])]
    unnamed x26 -> x14, local copies, waits for them, and re-layouts: 9.19 us -> 1.84 us
    ppermute x30 -> x18, starting transfers between devices: 19.8 us -> 13.9 us  [shifted(): return lax.ppermute(x, axis, [(i, (i + step) % size) for i in range(size)])]
    all_to_all x4, starting transfers between devices: 34.8 us -> 32.6 us  [exchanged(): return lax.all_to_all(tiles, ROW, split_axis=0, concat_axis=0, tiled=True)]
  transfers between devices with their start and end apart: 34 -> 22, of which waited for: 12 -> 12; matrix products, arithmetic and copies ran while one was open for 1% -> 1% of each run, Pallas kernels for 4% -> 22%
where the time goes in v2:
time: 198 us; the launch traced here: 197 us
  waiting for transfers between devices  89.4 us (45%)
  Pallas kernels  53.9 us (27%)
  starting transfers between devices  46.5 us (23%)
  local copies, waits for them, and re-layouts  4.46 us (2%)
  other arithmetic  2.32 us (1%)
    ppermute x18, waiting for transfers between devices, shifted(): return lax.ppermute(x, axis, [(i, (i + step) % size) for i in range(size)])  54.2 us
    pallas_call x8, Pallas kernels, call(): pl.pallas_call(kernel, out_shape=out, in_specs=ins, out_specs=outs, scrat...  53.9 us
    all_to_all x4, waiting for transfers between devices, exchanged(): return lax.all_to_all(tiles, ROW, split_axis=0, concat_axis=0, tiled=True)  35.2 us
    all_to_all x4, starting transfers between devices, exchanged(): return lax.all_to_all(tiles, ROW, split_axis=0, concat_axis=0, tiled=True)  32.6 us
    ppermute x18, starting transfers between devices, shifted(): return lax.ppermute(x, axis, [(i, (i + step) % size) for i in range(size)])  13.9 us
  transfers between devices with their start and end apart: 22, of which 12 were waited for; matrix products, arithmetic and copies ran while one was open for 1% of the time, Pallas kernels for 22%

profile of v2, /device:TPU:32, one launch (start us, length us, event | category | flops | bytes accessed | tf_op | source)
XLA Modules:
  0.0 196.9 jit_solution(14341724452088819956)
XLA Ops:
  1.7 2.8 %collective-permute-start.2 = (f32[2,512,256]{2,1,0:T(8,128)S(1)}, f32[2,512,256]{2,1,0:T(8,128)S(1)}, u32[]{:S(2)}, u32[]{:S(2)}) collective-permute-start(f32[2,512,256]{2,1,0:T(8,128)S(1)} %get-tuple-element.9.second_ref), channel_id=1, source_target_pairs={{0,6},{2,0},{4,2},{6,4},{1,7},{3,1},{5,3},{7,5},{8,14},{10,8},{12,... | collective-permute-start | bytes 3145736 | tf_op jit(solution)/shard_map/ppermute | solution.py:206
  5.4 4.1 %shard_map.42 = (f32[768,256]{1,0:T(8,128)S(1)}, f32[768,256]{1,0:T(8,128)S(1)}) custom-call(s32[2]{0:T(128)S(1)} %pad_add_fusion.place_ref, f32[2,512,256]{2,1,0:T(8,128)S(1)} %get-tuple-element.10.first_ref, f32[2,512,256]{2,1,0:T(8,128)S(1)} %get-tuple-element.9.second_ref), custom_call_target="tpu_custom_call" | custom-call | tf_op jit(solution)/shard_map/pallas_call | solution.py:200
  10.1 1.9 collective-permute-done.13
  12.0 2.5 %collective-permute-start.6 = (f32[2,512,256]{2,1,0:T(8,128)S(1)}, f32[2,512,256]{2,1,0:T(8,128)}, u32[]{:S(2)}, u32[]{:S(2)}) collective-permute-start(f32[2,512,256]{2,1,0:T(8,128)S(1)} %get-tuple-element.10.first_ref), channel_id=1, source_target_pairs={{0,6},{2,0},{4,2},{6,4},{1,7},{3,1},{5,3},{7,5},{8,14},{10,8},{12,... | collective-permute-start | bytes 3145736 | tf_op jit(solution)/shard_map/ppermute | solution.py:206
  14.5 13.5 %collective-permute-done.2.refs_2_.refs_5_ = f32[2,512,256]{2,1,0:T(8,128)S(1)} collective-permute-done((f32[2,512,256]{2,1,0:T(8,128)S(1)}, f32[2,512,256]{2,1,0:T(8,128)S(1)}, u32[]{:S(2)}, u32[]{:S(2)}) %collective-permute-start.2) | collective-permute-done | bytes 1048608 | tf_op jit(solution)/shard_map/ppermute | solution.py:206
  28.1 3.7 %collective-permute-start.10 = (f32[2,512,256]{2,1,0:T(8,128)S(1)}, f32[2,512,256]{2,1,0:T(8,128)}, u32[]{:S(2)}, u32[]{:S(2)}) collective-permute-start(f32[2,512,256]{2,1,0:T(8,128)S(1)} %collective-permute-done.2.refs_2_.refs_5_), channel_id=1, source_target_pairs={{0,6},{2,0},{4,2},{6,4},{1,7},{3,1},{5,3},{7,5},{8,14},{10,8},{12,... | collective-permute-start | bytes 3145736 | tf_op jit(solution)/shard_map/ppermute | solution.py:206
  31.9 21.1 %collective-permute-done.1.refs_1_.refs_2_ = f32[2,512,256]{2,1,0:T(8,128)} collective-permute-done((f32[2,512,256]{2,1,0:T(8,128)S(1)}, f32[2,512,256]{2,1,0:T(8,128)}, u32[]{:S(2)}, u32[]{:S(2)}) %collective-permute-start.1) | collective-permute-done | bytes 1048608 | tf_op jit(solution)/shard_map/ppermute | solution.py:206
  54.0 11.4 %all-to-all-start.2 = ((f32[32,24,256]{2,1,0:T(8,128)}), f32[32,24,256]{2,1,0:T(8,128)}, u32[]{:S(2)}, u32[]{:S(2)}) async-start(f32[32,24,256]{2,1,0:T(8,128)} %bitcast.4), calls=%async_computation.2 | async-start | bytes 1572864 | tf_op jit(solution)/shard_map/all_to_all | solution.py:219
  65.5 6.4 %collective-permute-done.10.refs_2_.refs_7_ = f32[2,512,256]{2,1,0:T(8,128)} collective-permute-done((f32[2,512,256]{2,1,0:T(8,128)S(1)}, f32[2,512,256]{2,1,0:T(8,128)}, u32[]{:S(2)}, u32[]{:S(2)}) %collective-permute-start.10) | collective-permute-done | bytes 1048608 | tf_op jit(solution)/shard_map/ppermute | solution.py:206
  72.4 5.8 %collective-permute-done.9.refs_1_.refs_6_ = f32[2,512,256]{2,1,0:T(8,128)} collective-permute-done((f32[2,512,256]{2,1,0:T(8,128)}, f32[2,512,256]{2,1,0:T(8,128)}, u32[]{:S(2)}, u32[]{:S(2)}) %collective-permute-start.9) | collective-permute-done | bytes 1048608 | tf_op jit(solution)/shard_map/ppermute | solution.py:206
  78.7 5.2 %shard_map.37.refs_0_ = f32[4,128,256]{2,1,0:T(8,128)} custom-call(s32[2]{0:T(128)} %copy-done, f32[4096,128]{1,0:T(8,128)} %field_ref.1, f32[4,512,256]{2,1,0:T(8,128)} %refs_1_.3, f32[4,512,256]{2,1,0:T(8,128)} %refs_1_.3, f32[4,512,256]{2,1,0:T(8,128)} %collective-permute-done.refs_2_.refs_3_.refs_8_.refs_9_, ...), custom_call_target="tpu_custom_call" | custom-call | tf_op jit(solution)/shard_map/pallas_call | solution.py:200
  85.0 7.1 %shard_map.38.refs_0_ = f32[4,128,256]{2,1,0:T(8,128)} custom-call(s32[2]{0:T(128)} %copy-done, f32[4096,128]{1,0:T(8,128)} %field_ref.1, f32[4,128,256]{2,1,0:T(8,128)} %shard_map.37.refs_0_, f32[2,512,256]{2,1,0:T(8,128)} %collective-permute-done.1.refs_1_.refs_2_, f32[2,512,256]{2,1,0:T(8,128)} %copy-done.1, f32[2,512,256]{2,1,0:T(8,128)} %copy-done.3, ...), custom_call_target="tpu_custom_call" | custom-call | tf_op jit(solution)/shard_map/pallas_call | solution.py:200
  92.1 7.1 %shard_map.39.refs_0_ = f32[4,128,256]{2,1,0:T(8,128)} custom-call(s32[2]{0:T(128)} %copy-done, f32[4096,128]{1,0:T(8,128)} %field_ref.1, f32[4,128,256]{2,1,0:T(8,128)} %shard_map.38.refs_0_, f32[2,512,256]{2,1,0:T(8,128)} %collective-permute-done.5.refs_1_.refs_3_, f32[2,512,256]{2,1,0:T(8,128)} %collective-permute-done.6.refs_2_.refs_4_, ...), custom_call_target="tpu_custom_call" | custom-call | tf_op jit(solution)/shard_map/pallas_call | solution.py:200
  99.3 6.8 %shard_map.40 = f32[32,32,128]{2,1,0:T(8,128)} custom-call(s32[2]{0:T(128)} %copy-done, f32[4096,128]{1,0:T(8,128)} %field_ref.1, f32[4,128,256]{2,1,0:T(8,128)} %shard_map.39.refs_0_, f32[2,512,256]{2,1,0:T(8,128)} %collective-permute-done.9.refs_1_.refs_6_, f32[2,512,256]{2,1,0:T(8,128)} %collective-permute-done.10.refs_2_.refs_7_, ...), custom_call_target="tpu_custom_call" | custom-call | tf_op jit(solution)/shard_map/pallas_call | solution.py:200
  106.0 11.4 %all-to-all-start = ((f32[32,32,128]{2,1,0:T(8,128)}), f32[32,32,128]{2,1,0:T(8,128)S(1)}, u32[]{:S(2)}, u32[]{:S(2)}) async-start(f32[32,32,128]{2,1,0:T(8,128)} %shard_map.40), calls=%async_computation | async-start | bytes 1048576 | tf_op jit(solution)/shard_map/all_to_all | solution.py:219
  118.7 2.0 %collective-permute-start.15 = (f32[24,256]{1,0:T(8,128)S(1)}, f32[24,256]{1,0:T(8,128)S(1)}, u32[]{:S(2)}, u32[]{:S(2)}) collective-permute-start(f32[24,256]{1,0:T(8,128)S(1)} %reduce_sum.9), channel_id=1, source_target_pairs={{0,2},{2,4},{4,6},{6,0},{1,3},{3,5},{5,7},{7,1},{8,10},{10,12},{12... | collective-permute-start | bytes 73736 | tf_op jit(solution)/shard_map/ppermute | solution.py:206
  124.1 2.0 collective-permute-done.14
  126.1 9.2 %all-to-all-done.arrived_ref = f32[32,32,128]{2,1,0:T(8,128)S(1)} async-done(((f32[32,32,128]{2,1,0:T(8,128)}), f32[32,32,128]{2,1,0:T(8,128)S(1)}, u32[]{:S(2)}, u32[]{:S(2)}) %all-to-all-start) | async-done | bytes 524320 | tf_op jit(solution)/shard_map/all_to_all | solution.py:219
  136.2 4.8 %all-to-all-start.3 = ((f32[32,24,256]{2,1,0:T(8,128)}), f32[32,24,256]{2,1,0:T(8,128)S(1)}, u32[]{:S(2)}, u32[]{:S(2)}) async-start(f32[32,24,256]{2,1,0:T(8,128)} %broadcast_in_dim.3), calls=%async_computation.3 | async-start | bytes 1572864 | tf_op jit(solution)/shard_map/all_to_all | solution.py:219
  141.9 21.6 %all-to-all-done.3 = f32[32,24,256]{2,1,0:T(8,128)S(1)} async-done(((f32[32,24,256]{2,1,0:T(8,128)}), f32[32,24,256]{2,1,0:T(8,128)S(1)}, u32[]{:S(2)}, u32[]{:S(2)}) %all-to-all-start.3) | async-done | bytes 786464 | tf_op jit(solution)/shard_map/all_to_all | solution.py:219
  163.5 4.9 %all-to-all-start.1 = ((f32[32,32,128]{2,1,0:T(8,128)}), f32[32,32,128]{2,1,0:T(8,128)S(1)}, u32[]{:S(2)}, u32[]{:S(2)}) async-start(f32[32,32,128]{2,1,0:T(8,128)} %shard_map.41), calls=%async_computation.1 | async-start | bytes 1048576 | tf_op jit(solution)/shard_map/all_to_all | solution.py:219
  168.7 11.9 %shard_map.43.held_ref = bf16[8,4,2,512,256]{4,3,2,1,0:T(8,128)(2,1)} custom-call(f32[4,512,256]{2,1,0:T(8,128)} %refs_1_.3, f32[4,512,256]{2,1,0:T(8,128)} %refs_1_.3, f32[2,512,256]{2,1,0:T(8,128)} %collective-permute-done.1.refs_1_.refs_2_, f32[2,512,256]{2,1,0:T(8,128)} %collective-permute-done.5.refs_1_.refs_3_, ...), custom_call_target="tpu_custom_call" | custom-call | tf_op jit(solution)/shard_map/pallas_call | solution.py:200
  180.7 4.5 %all-to-all-done.1.sums_ref = f32[32,32,128]{2,1,0:T(8,128)S(1)} async-done(((f32[32,32,128]{2,1,0:T(8,128)}), f32[32,32,128]{2,1,0:T(8,128)S(1)}, u32[]{:S(2)}, u32[]{:S(2)}) %all-to-all-start.1) | async-done | bytes 524320 | tf_op jit(solution)/shard_map/all_to_all | solution.py:219
  186.0 10.7 %shard_map.44 = f32[4096,128]{1,0:T(8,128)} custom-call(s32[2]{0:T(128)} %copy-done, f32[4096,128]{1,0:T(8,128)} %field_ref.1, f32[4,256,256]{2,1,0:T(8,128)} %factors_ref.1, f32[32,32,128]{2,1,0:T(8,128)} %copy-done.5, f32[768,256]{1,0:T(8,128)} %bitcast.6, f32[768,256]{1,0:T(8,128)} %copy-done.6, bf16[8,4,2,512,256]{4,3,2,1,0:T(8,128)(2,1)} %shard_map.43.held_ref), custom_call_target="tpu_custom_call" | custom-call | tf_op jit(solution)/shard_map/pallas_call | solution.py:200
  (48 shorter events, 14.0 us)
Async XLA Ops:
  1.7 26.4 %collective-permute-start.2 = (f32[2,512,256]{2,1,0:T(8,128)S(1)}, f32[2,512,256]{2,1,0:T(8,128)S(1)}, u32[]{:S(2)}, u32[]{:S(2)}) collective-permute-start(f32[2,512,256]{2,1,0:T(8,128)S(1)} %get-tuple-element.9.second_ref), channel_id=1, source_target_pairs={{0,6},{2,0},{4,2},{6,4},{1,7},{3,1},{5,3},{7,5},{8,14},{10,8},{12,... | collective-permute-start | bytes 3145736 | tf_op jit(solution)/shard_map/ppermute | solution.py:206
  4.5 27.3 %collective-permute-start.5 = (f32[2,512,256]{2,1,0:T(8,128)S(1)}, f32[2,512,256]{2,1,0:T(8,128)}, u32[]{:S(2)}, u32[]{:S(2)}) collective-permute-start(f32[2,512,256]{2,1,0:T(8,128)S(1)} %get-tuple-element.9.second_ref), channel_id=1, source_target_pairs={{0,2},{2,4},{4,6},{6,0},{1,3},{3,5},{5,7},{7,1},{8,10},{10,12},{12... | collective-permute-start | bytes 3145736 | tf_op jit(solution)/shard_map/ppermute | solution.py:206
  4.5 48.4 %collective-permute-start.1 = (f32[2,512,256]{2,1,0:T(8,128)S(1)}, f32[2,512,256]{2,1,0:T(8,128)}, u32[]{:S(2)}, u32[]{:S(2)}) collective-permute-start(f32[2,512,256]{2,1,0:T(8,128)S(1)} %get-tuple-element.10.first_ref), channel_id=1, source_target_pairs={{0,2},{2,4},{4,6},{6,0},{1,3},{3,5},{5,7},{7,1},{8,10},{10,12},{12... | collective-permute-start | bytes 3145736 | tf_op jit(solution)/shard_map/ppermute | solution.py:206
  5.3 72.9 %collective-permute-start = (f32[4,512,256]{2,1,0:T(8,128)}, f32[4,512,256]{2,1,0:T(8,128)}, u32[]{:S(2)}, u32[]{:S(2)}) collective-permute-start(f32[4,512,256]{2,1,0:T(8,128)} %refs_1_.3), channel_id=1, source_target_pairs={{0,1},{1,0},{2,3},{3,2},{4,5},{5,4},{6,7},{7,6},{8,9},{9,8},{10,11... | collective-permute-start | bytes 6291464 | tf_op jit(solution)/shard_map/ppermute | solution.py:206
  5.4 48.6 %copy-start = (s32[2]{0:T(128)}, s32[2]{0:T(128)S(1)}, u32[]{:S(2)}) copy-start(s32[2]{0:T(128)S(1)} %pad_add_fusion.place_ref) | copy-start | bytes 28
  9.5 2.5 %collective-permute-start.13 = (f32[768,256]{1,0:T(8,128)S(1)}, f32[768,256]{1,0:T(8,128)S(1)}, u32[]{:S(2)}, u32[]{:S(2)}) collective-permute-start(f32[768,256]{1,0:T(8,128)S(1)} %get-tuple-element.8), channel_id=1, source_target_pairs={{0,1},{1,0},{2,3},{3,2},{4,5},{5,4},{6,7},{7,6},{8,9},{9,8},{10,11... | collective-permute-start | bytes 2359304 | tf_op jit(solution)/shard_map/ppermute | solution.py:206
  12.0 53.4 %collective-permute-start.6 = (f32[2,512,256]{2,1,0:T(8,128)S(1)}, f32[2,512,256]{2,1,0:T(8,128)}, u32[]{:S(2)}, u32[]{:S(2)}) collective-permute-start(f32[2,512,256]{2,1,0:T(8,128)S(1)} %get-tuple-element.10.first_ref), channel_id=1, source_target_pairs={{0,6},{2,0},{4,2},{6,4},{1,7},{3,1},{5,3},{7,5},{8,14},{10,8},{12,... | collective-permute-start | bytes 3145736 | tf_op jit(solution)/shard_map/ppermute | solution.py:206
  28.1 55.9 %copy-start.1 = (f32[2,512,256]{2,1,0:T(8,128)}, f32[2,512,256]{2,1,0:T(8,128)S(1)}, u32[]{:S(2)}) copy-start(f32[2,512,256]{2,1,0:T(8,128)S(1)} %collective-permute-done.2.refs_2_.refs_5_) | copy-start | bytes 3145732
  28.1 43.8 %collective-permute-start.10 = (f32[2,512,256]{2,1,0:T(8,128)S(1)}, f32[2,512,256]{2,1,0:T(8,128)}, u32[]{:S(2)}, u32[]{:S(2)}) collective-permute-start(f32[2,512,256]{2,1,0:T(8,128)S(1)} %collective-permute-done.2.refs_2_.refs_5_), channel_id=1, source_target_pairs={{0,6},{2,0},{4,2},{6,4},{1,7},{3,1},{5,3},{7,5},{8,14},{10,8},{12,... | collective-permute-start | bytes 3145736 | tf_op jit(solution)/shard_map/ppermute | solution.py:206
  31.9 40.0 %collective-permute-start.4 = (f32[2,512,256]{2,1,0:T(8,128)S(1)}, f32[2,512,256]{2,1,0:T(8,128)S(1)}, u32[]{:S(2)}, u32[]{:S(2)}) collective-permute-start(f32[2,512,256]{2,1,0:T(8,128)S(1)} %collective-permute-done.2.refs_2_.refs_5_), channel_id=1, source_target_pairs={{0,1},{1,0},{2,3},{3,2},{4,5},{5,4},{6,7},{7,6},{8,9},{9,8},{10,11... | collective-permute-start | bytes 3145736 | tf_op jit(solution)/shard_map/ppermute | solution.py:206
  52.9 25.3 %collective-permute-start.9 = (f32[2,512,256]{2,1,0:T(8,128)}, f32[2,512,256]{2,1,0:T(8,128)}, u32[]{:S(2)}, u32[]{:S(2)}) collective-permute-start(f32[2,512,256]{2,1,0:T(8,128)} %collective-permute-done.1.refs_1_.refs_2_), channel_id=1, source_target_pairs={{0,2},{2,4},{4,6},{6,0},{1,3},{3,5},{5,7},{7,1},{8,10},{10,12},{12... | collective-permute-start | bytes 3145736 | tf_op jit(solution)/shard_map/ppermute | solution.py:206
  54.0 52.1 %all-to-all-start.2 = ((f32[32,24,256]{2,1,0:T(8,128)}), f32[32,24,256]{2,1,0:T(8,128)}, u32[]{:S(2)}, u32[]{:S(2)}) async-start(f32[32,24,256]{2,1,0:T(8,128)} %bitcast.4), calls=%async_computation.2 | async-start | bytes 1572864 | tf_op jit(solution)/shard_map/all_to_all | solution.py:219
  65.4 18.6 %collective-permute-start.3 = (f32[2,512,256]{2,1,0:T(8,128)}, f32[2,512,256]{2,1,0:T(8,128)S(1)}, u32[]{:S(2)}, u32[]{:S(2)}) collective-permute-start(f32[2,512,256]{2,1,0:T(8,128)} %collective-permute-done.1.refs_1_.refs_2_), channel_id=1, source_target_pairs={{0,1},{1,0},{2,3},{3,2},{4,5},{5,4},{6,7},{7,6},{8,9},{9,8},{10,11... | collective-permute-start | bytes 3145736 | tf_op jit(solution)/shard_map/ppermute | solution.py:206
  71.9 20.2 %collective-permute-start.7 = (f32[2,512,256]{2,1,0:T(8,128)}, f32[2,512,256]{2,1,0:T(8,128)}, u32[]{:S(2)}, u32[]{:S(2)}) collective-permute-start(f32[2,512,256]{2,1,0:T(8,128)} %collective-permute-done.5.refs_1_.refs_3_), channel_id=1, source_target_pairs={{0,1},{1,0},{2,3},{3,2},{4,5},{5,4},{6,7},{7,6},{8,9},{9,8},{10,11... | collective-permute-start | bytes 3145736 | tf_op jit(solution)/shard_map/ppermute | solution.py:206
  71.9 20.2 %collective-permute-start.8 = (f32[2,512,256]{2,1,0:T(8,128)}, f32[2,512,256]{2,1,0:T(8,128)}, u32[]{:S(2)}, u32[]{:S(2)}) collective-permute-start(f32[2,512,256]{2,1,0:T(8,128)} %collective-permute-done.6.refs_2_.refs_4_), channel_id=1, source_target_pairs={{0,1},{1,0},{2,3},{3,2},{4,5},{5,4},{6,7},{7,6},{8,9},{9,8},{10,11... | collective-permute-start | bytes 3145736 | tf_op jit(solution)/shard_map/ppermute | solution.py:206
  78.2 21.0 %collective-permute-start.12 = (f32[2,512,256]{2,1,0:T(8,128)}, f32[2,512,256]{2,1,0:T(8,128)}, u32[]{:S(2)}, u32[]{:S(2)}) collective-permute-start(f32[2,512,256]{2,1,0:T(8,128)} %collective-permute-done.10.refs_2_.refs_7_), channel_id=1, source_target_pairs={{0,1},{1,0},{2,3},{3,2},{4,5},{5,4},{6,7},{7,6},{8,9},{9,8},{10,11... | collective-permute-start | bytes 3145736 | tf_op jit(solution)/shard_map/ppermute | solution.py:206
  78.2 21.0 %collective-permute-start.11 = (f32[2,512,256]{2,1,0:T(8,128)}, f32[2,512,256]{2,1,0:T(8,128)}, u32[]{:S(2)}, u32[]{:S(2)}) collective-permute-start(f32[2,512,256]{2,1,0:T(8,128)} %collective-permute-done.9.refs_1_.refs_6_), channel_id=1, source_target_pairs={{0,1},{1,0},{2,3},{3,2},{4,5},{5,4},{6,7},{7,6},{8,9},{9,8},{10,11... | collective-permute-start | bytes 3145736 | tf_op jit(solution)/shard_map/ppermute | solution.py:206
  106.0 29.2 %all-to-all-start = ((f32[32,32,128]{2,1,0:T(8,128)}), f32[32,32,128]{2,1,0:T(8,128)S(1)}, u32[]{:S(2)}, u32[]{:S(2)}) async-start(f32[32,32,128]{2,1,0:T(8,128)} %shard_map.40), calls=%async_computation | async-start | bytes 1048576 | tf_op jit(solution)/shard_map/all_to_all | solution.py:219
  118.6 3.9 %collective-permute-start.16 = (f32[24,256]{1,0:T(8,128)S(1)}, f32[24,256]{1,0:T(8,128)S(1)}, u32[]{:S(2)}, u32[]{:S(2)}) collective-permute-start(f32[24,256]{1,0:T(8,128)S(1)} %reduce_sum.9), channel_id=1, source_target_pairs={{0,6},{2,0},{4,2},{6,4},{1,7},{3,1},{5,3},{7,5},{8,14},{10,8},{12,... | collective-permute-start | bytes 73736 | tf_op jit(solution)/shard_map/ppermute | solution.py:206
  118.7 5.4 %collective-permute-start.15 = (f32[24,256]{1,0:T(8,128)S(1)}, f32[24,256]{1,0:T(8,128)S(1)}, u32[]{:S(2)}, u32[]{:S(2)}) collective-permute-start(f32[24,256]{1,0:T(8,128)S(1)} %reduce_sum.9), channel_id=1, source_target_pairs={{0,2},{2,4},{4,6},{6,0},{1,3},{3,5},{5,7},{7,1},{8,10},{10,12},{12... | collective-permute-start | bytes 73736 | tf_op jit(solution)/shard_map/ppermute | solution.py:206
  120.7 5.3 %collective-permute-start.14 = (f32[24,256]{1,0:T(8,128)S(1)}, f32[24,256]{1,0:T(8,128)S(1)}, u32[]{:S(2)}, u32[]{:S(2)}) collective-permute-start(f32[24,256]{1,0:T(8,128)S(1)} %reduce_sum.9), channel_id=1, source_target_pairs={{0,4},{2,6},{4,0},{6,2},{1,5},{3,7},{5,1},{7,3},{8,12},{10,14},{12... | collective-permute-start | bytes 73736 | tf_op jit(solution)/shard_map/ppermute | solution.py:206
  136.2 27.3 %all-to-all-start.3 = ((f32[32,24,256]{2,1,0:T(8,128)}), f32[32,24,256]{2,1,0:T(8,128)S(1)}, u32[]{:S(2)}, u32[]{:S(2)}) async-start(f32[32,24,256]{2,1,0:T(8,128)} %broadcast_in_dim.3), calls=%async_computation.3 | async-start | bytes 1572864 | tf_op jit(solution)/shard_map/all_to_all | solution.py:219
  163.5 21.7 %all-to-all-start.1 = ((f32[32,32,128]{2,1,0:T(8,128)}), f32[32,32,128]{2,1,0:T(8,128)S(1)}, u32[]{:S(2)}, u32[]{:S(2)}) async-start(f32[32,32,128]{2,1,0:T(8,128)} %shard_map.41), calls=%async_computation.1 | async-start | bytes 1048576 | tf_op jit(solution)/shard_map/all_to_all | solution.py:219
  168.4 12.3 %collective-permute-start.17 = (f32[768,256]{1,0:T(8,128)S(1)}, f32[768,256]{1,0:T(8,128)S(1)}, u32[]{:S(2)}, u32[]{:S(2)}) collective-permute-start(f32[768,256]{1,0:T(8,128)S(1)} %bitcast.5), channel_id=1, source_target_pairs={{0,1},{1,0},{2,3},{3,2},{4,5},{5,4},{6,7},{7,6},{8,9},{9,8},{10,11... | collective-permute-start | bytes 2359304 | tf_op jit(solution)/shard_map/ppermute | solution.py:206
  (5 other events, 35.6 us)

commit v3 on v2

--- a/solution.py
+++ b/solution.py
@@ -131,14 +131,14 @@
     out(7).wait()
 
 
-def last_kernel(place_ref, field_ref, factors_ref, sums_ref, mine_ref, other_ref, held_ref, out_ref,
-                field, new, factors, sums, mine, other, held, sems, out_sems):
+def last_kernel(place_ref, field_ref, factors_ref, sums, mine_ref, other_ref, held_ref, out_ref,
+                field, new, factors, mine, other, held, sems, out_sems):
     where = starts(place_ref)
-    pairs = [(sums_ref, sums), (factors_ref, factors), (mine_ref, mine), (other_ref, other)]
+    pairs = [(factors_ref, factors), (mine_ref, mine), (other_ref, other)]
     for block in range(8):
         pairs += [(field_ref.at[pl.ds(where[block], ROWS), :], field.at[block]), (held_ref.at[block], held.at[block])]
     copies = fetch(pairs, sems)
-    for copy in copies[:4]:
+    for copy in copies[:3]:
         copy.wait()
 
     def gram(k, j):
@@ -146,19 +146,16 @@
         rows = pl.ds(256 * at, 256)
         return jnp.where(place_ref[1] == half, mine[rows, :], other[rows, :])
 
-    coeffs = []
+    lefts, parts = [sums[:, 8 * k : 8 * k + 8, :].reshape(256, 128) for k in range(4)], []
     for k in range(4):
-        left = sums[:, 8 * k : 8 * k + 8, :].reshape(256, 128)
-        for j in range(k):
-            left = left - product(gram(k, j), coeffs[j])
-        coeffs.append(product(factors[k], left))
-    parts = []
-    for high, low in map(halves, coeffs):
+        for i in range(k + 1, 4):
+            lefts[i] = lefts[i] - product(gram(i, k), lefts[k])
+        high, low = halves(product(factors[k], lefts[k]))
         parts.append((jnp.concatenate([high, low], axis=1), high))
     outs = []
     for block in range(8):
+        copies[3 + 2 * block].wait()
         copies[4 + 2 * block].wait()
-        copies[5 + 2 * block].wait()
         total = None
         for k, (wide, high) in enumerate(parts):
             both = dot(held[block, k, 0], wide)
@@ -171,13 +168,17 @@
         copy.wait()
 
 
-def gram_kernel(place_ref, first_ref, second_ref, mine_ref, other_ref):
+def gram_kernel(place_ref, first_ref, second_ref, factors_ref, mine_ref, other_ref):
     panels = [first_ref[0], first_ref[1], second_ref[0], second_ref[1]]
-    parts = [halves(panel) for panel in panels[:3]]
+    scaled = []
+    for j in range(3):
+        vh, vl = halves(panels[j])
+        th, tl = halves(factors_ref[j])
+        scaled.append(halves(dot(vh, th) + dot(vh, tl) + dot(vl, th)))
     for k in range(1, 4):
         lh, ll = halves(panels[k].T)
         for j in range(k):
-            high, low = parts[j]
+            high, low = scaled[j]
             block = dot(lh, high) + dot(lh, low) + dot(ll, high)
             half, at = divmod(BLOCKS.index((k, j)), 3)
 
@@ -225,9 +226,9 @@
     return exchanged(copies)
 
 
-def gram(pairs, place):
+def gram(pairs, factors, place):
     share = jax.ShapeDtypeStruct((768, 256), F32)
-    mine, other = call(gram_kernel, [share, share], [SMEM, VMEM, VMEM], [VMEM, VMEM], [], place, *pairs)
+    mine, other = call(gram_kernel, [share, share], [SMEM] + [VMEM] * 3, [VMEM, VMEM], [], place, *pairs, factors)
     mine = mine + shifted(other, "core", 1)
     part = exchanged(mine.reshape(32, 24, 256)).sum(axis=0)
     part = (part + shifted(part, "x", 2)) + (shifted(part, "x", 1) + shifted(part, "x", -1))
@@ -242,7 +243,7 @@
     own = [reflectors[:2], reflectors[2:]]
     swapped = shifted(reflectors, "core", 1)
     moving = [gathered(pair, own[pair]) for pair in range(2)]
-    mine, other = gram(own, place)
+    mine, other = gram(own, factors, place)
     piece = lambda block, pair: {0: reflectors, 4: swapped}.get(block, moving[pair].get(block))
     everything = [piece(block, pair) for block in range(8) for pair in range(2)]
 
@@ -252,7 +253,7 @@
                     [SMEM, ANY] + [ANY] * (len(olds) + len(items)), VMEM if last else ANY,
                     [pltpu.VMEM((count, ROWS, 128), F32), pltpu.VMEM((2 * len(items), ROWS, 256), F32),
                      pltpu.VMEM((4, 128, 256), F32), sem((count + 2 * len(items) + 1,))],
-                    place, eigvecs, *olds, *[piece(*item) for item in items])
+                    place, eigvecs, *olds, *[piece(*item) for item in items], limit=24 if last else None)
 
     sums, tiles = jax.ShapeDtypeStruct((4, 128, 256), F32), jax.ShapeDtypeStruct((32, 32, 128), F32)
     state = stage(((0, 0), (0, 1), (4, 0), (4, 1)), [], sums)
@@ -264,9 +265,9 @@
                 [pltpu.VMEM((3, 4, ROWS, 256), F32), pltpu.VMEM((2, 4, 2, ROWS, 256), BF16), sem((3, 4)), sem((2,))], *everything)
     block = pltpu.VMEM((8, ROWS, 128), F32)
     share = pltpu.VMEM((768, 256), F32)
-    return call(last_kernel, jax.ShapeDtypeStruct((4096, 128), F32), [SMEM] + [ANY] * 6, ANY,
-                [block, block, pltpu.VMEM((4, 256, 256), F32), pltpu.VMEM((32, 32, 128), F32), share, share,
-                 pltpu.VMEM((8, 4, 2, ROWS, 256), BF16), sem((20,)), sem((8,))],
+    return call(last_kernel, jax.ShapeDtypeStruct((4096, 128), F32), [SMEM, ANY, ANY, VMEM, ANY, ANY, ANY], ANY,
+                [block, block, pltpu.VMEM((4, 256, 256), F32), share, share,
+                 pltpu.VMEM((8, 4, 2, ROWS, 256), BF16), sem((19,)), sem((8,))],
                 place, eigvecs, factors, sums, mine, other, held)
 
 

time: 198 us -> 197 us (level)
  Pallas kernels: 53.9 us -> 51.8 us
    pallas_call x8, Pallas kernels: 53.9 us -> 51.8 us  [call(): pl.pallas_call(kernel, out_shape=out, in_specs=ins, out_specs=outs, scrat...]
  transfers between devices with their start and end apart: 22 -> 22, of which waited for: 12 -> 11; matrix products, arithmetic and copies ran while one was open for 1% -> 1% of each run, Pallas kernels for 22% -> 21%
where the time goes in v3:
time: 197 us; the launch traced here: 196 us
  waiting for transfers between devices  88.8 us (45%)
  Pallas kernels  51.8 us (26%)
  starting transfers between devices  46.6 us (24%)
  local copies, waits for them, and re-layouts  6.32 us (3%)
  other arithmetic  2.29 us (1%)
    ppermute x18, waiting for transfers between devices, shifted(): return lax.ppermute(x, axis, [(i, (i + step) % size) for i in range(size)])  53.6 us
    pallas_call x8, Pallas kernels, call(): pl.pallas_call(kernel, out_shape=out, in_specs=ins, out_specs=outs, scrat...  51.8 us
    all_to_all x4, waiting for transfers between devices, exchanged(): return lax.all_to_all(tiles, ROW, split_axis=0, concat_axis=0, tiled=True)  35.2 us
    all_to_all x4, starting transfers between devices, exchanged(): return lax.all_to_all(tiles, ROW, split_axis=0, concat_axis=0, tiled=True)  32.5 us
    ppermute x18, starting transfers between devices, shifted(): return lax.ppermute(x, axis, [(i, (i + step) % size) for i in range(size)])  14 us
  transfers between devices with their start and end apart: 22, of which 11 were waited for; matrix products, arithmetic and copies ran while one was open for 1% of the time, Pallas kernels for 21%

profile of v3, /device:TPU:32, one launch (start us, length us, event | category | flops | bytes accessed | tf_op | source)
XLA Modules:
  0.0 196.2 jit_solution(2022423627725688457)
XLA Ops:
  1.8 2.8 %collective-permute-start.2 = (f32[2,512,256]{2,1,0:T(8,128)S(1)}, f32[2,512,256]{2,1,0:T(8,128)}, u32[]{:S(2)}, u32[]{:S(2)}) collective-permute-start(f32[2,512,256]{2,1,0:T(8,128)S(1)} %get-tuple-element.9.second_ref), channel_id=1, source_target_pairs={{0,6},{2,0},{4,2},{6,4},{1,7},{3,1},{5,3},{7,5},{8,14},{10,8},{12,... | collective-permute-start | bytes 3145736 | tf_op jit(solution)/shard_map/ppermute | solution.py:207
  5.4 4.7 %shard_map.42 = (f32[768,256]{1,0:T(8,128)S(1)}, f32[768,256]{1,0:T(8,128)S(1)}) custom-call(s32[2]{0:T(128)S(1)} %pad_add_fusion.place_ref, f32[2,512,256]{2,1,0:T(8,128)S(1)} %get-tuple-element.10.first_ref, f32[2,512,256]{2,1,0:T(8,128)S(1)} %get-tuple-element.9.second_ref, f32[4,256,256]{2,1,0:T(8,128)S(1)} %copy-done.2), custom_call_target="tpu_custom_call" | custom-call | tf_op jit(solution)/shard_map/pallas_call | solution.py:201
  10.7 1.9 collective-permute-done.13
  12.6 2.5 %collective-permute-start.6 = (f32[2,512,256]{2,1,0:T(8,128)S(1)}, f32[2,512,256]{2,1,0:T(8,128)}, u32[]{:S(2)}, u32[]{:S(2)}) collective-permute-start(f32[2,512,256]{2,1,0:T(8,128)S(1)} %get-tuple-element.10.first_ref), channel_id=1, source_target_pairs={{0,6},{2,0},{4,2},{6,4},{1,7},{3,1},{5,3},{7,5},{8,14},{10,8},{12,... | collective-permute-start | bytes 3145736 | tf_op jit(solution)/shard_map/ppermute | solution.py:207
  15.1 13.0 %collective-permute-done.2.refs_2_.refs_5_ = f32[2,512,256]{2,1,0:T(8,128)} collective-permute-done((f32[2,512,256]{2,1,0:T(8,128)S(1)}, f32[2,512,256]{2,1,0:T(8,128)}, u32[]{:S(2)}, u32[]{:S(2)}) %collective-permute-start.2) | collective-permute-done | bytes 1048608 | tf_op jit(solution)/shard_map/ppermute | solution.py:207
  28.2 3.8 %collective-permute-start.10 = (f32[2,512,256]{2,1,0:T(8,128)}, f32[2,512,256]{2,1,0:T(8,128)S(1)}, u32[]{:S(2)}, u32[]{:S(2)}) collective-permute-start(f32[2,512,256]{2,1,0:T(8,128)} %collective-permute-done.2.refs_2_.refs_5_), channel_id=1, source_target_pairs={{0,6},{2,0},{4,2},{6,4},{1,7},{3,1},{5,3},{7,5},{8,14},{10,8},{12,... | collective-permute-start | bytes 3145736 | tf_op jit(solution)/shard_map/ppermute | solution.py:207
  32.0 21.1 %collective-permute-done.1.refs_1_.refs_2_ = f32[2,512,256]{2,1,0:T(8,128)} collective-permute-done((f32[2,512,256]{2,1,0:T(8,128)S(1)}, f32[2,512,256]{2,1,0:T(8,128)}, u32[]{:S(2)}, u32[]{:S(2)}) %collective-permute-start.1) | collective-permute-done | bytes 1048608 | tf_op jit(solution)/shard_map/ppermute | solution.py:207
  54.0 11.4 %all-to-all-start.2 = ((f32[32,24,256]{2,1,0:T(8,128)}), f32[32,24,256]{2,1,0:T(8,128)}, u32[]{:S(2)}, u32[]{:S(2)}) async-start(f32[32,24,256]{2,1,0:T(8,128)} %bitcast.4), calls=%async_computation.2 | async-start | bytes 1572864 | tf_op jit(solution)/shard_map/all_to_all | solution.py:220
  65.6 6.5 %collective-permute-done.10.refs_2_.refs_7_ = f32[2,512,256]{2,1,0:T(8,128)S(1)} collective-permute-done((f32[2,512,256]{2,1,0:T(8,128)}, f32[2,512,256]{2,1,0:T(8,128)S(1)}, u32[]{:S(2)}, u32[]{:S(2)}) %collective-permute-start.10) | collective-permute-done | bytes 1048608 | tf_op jit(solution)/shard_map/ppermute | solution.py:207
  72.6 5.7 %collective-permute-done.9.refs_1_.refs_6_ = f32[2,512,256]{2,1,0:T(8,128)} collective-permute-done((f32[2,512,256]{2,1,0:T(8,128)}, f32[2,512,256]{2,1,0:T(8,128)}, u32[]{:S(2)}, u32[]{:S(2)}) %collective-permute-start.9) | collective-permute-done | bytes 1048608 | tf_op jit(solution)/shard_map/ppermute | solution.py:207
  78.8 5.2 %shard_map.37.refs_0_ = f32[4,128,256]{2,1,0:T(8,128)} custom-call(s32[2]{0:T(128)} %copy-done.5, f32[4096,128]{1,0:T(8,128)} %field_ref.1, f32[4,512,256]{2,1,0:T(8,128)} %refs_1_.3, f32[4,512,256]{2,1,0:T(8,128)} %refs_1_.3, f32[4,512,256]{2,1,0:T(8,128)} %collective-permute-done.refs_2_.refs_3_.refs_8_.refs_9_, ...), custom_call_target="tpu_custom_call" | custom-call | tf_op jit(solution)/shard_map/pallas_call | solution.py:201
  85.0 7.2 %shard_map.38.refs_0_ = f32[4,128,256]{2,1,0:T(8,128)} custom-call(s32[2]{0:T(128)} %copy-done.5, f32[4096,128]{1,0:T(8,128)} %field_ref.1, f32[4,128,256]{2,1,0:T(8,128)} %shard_map.37.refs_0_, f32[2,512,256]{2,1,0:T(8,128)} %collective-permute-done.1.refs_1_.refs_2_, f32[2,512,256]{2,1,0:T(8,128)} %collective-permute-done.2.refs_2_.refs_5_, ...), custom_call_target="tpu_custom_call" | custom-call | tf_op jit(solution)/shard_map/pallas_call | solution.py:201
  92.3 7.3 %shard_map.39.refs_0_ = f32[4,128,256]{2,1,0:T(8,128)} custom-call(s32[2]{0:T(128)} %copy-done.5, f32[4096,128]{1,0:T(8,128)} %field_ref.1, f32[4,128,256]{2,1,0:T(8,128)} %shard_map.38.refs_0_, f32[2,512,256]{2,1,0:T(8,128)} %collective-permute-done.5.refs_1_.refs_3_, f32[2,512,256]{2,1,0:T(8,128)} %collective-permute-done.6.refs_2_.refs_4_, ...), custom_call_target="tpu_custom_call" | custom-call | tf_op jit(solution)/shard_map/pallas_call | solution.py:201
  100.6 4.3 %shard_map.40 = f32[32,32,128]{2,1,0:T(8,128)S(1)} custom-call(s32[2]{0:T(128)S(1)} %copy-done.6, f32[4096,128]{1,0:T(8,128)S(1)} %copy-done, f32[4,128,256]{2,1,0:T(8,128)S(1)} %copy-done.4, f32[2,512,256]{2,1,0:T(8,128)} %collective-permute-done.9.refs_1_.refs_6_, f32[2,512,256]{2,1,0:T(8,128)S(1)} %collective-permute-done.10.refs_2_.refs_7_, ...), custom_call_target="tpu_custom_call" | custom-call | tf_op jit(solution)/shard_map/pallas_call | solution.py:201
  105.7 11.4 %all-to-all-start = ((f32[32,32,128]{2,1,0:T(8,128)}), f32[32,32,128]{2,1,0:T(8,128)S(1)}, u32[]{:S(2)}, u32[]{:S(2)}) async-start(f32[32,32,128]{2,1,0:T(8,128)} %copy-done.3), calls=%async_computation | async-start | bytes 1048576 | tf_op jit(solution)/shard_map/all_to_all | solution.py:220
  118.4 2.0 %collective-permute-start.15 = (f32[24,256]{1,0:T(8,128)S(1)}, f32[24,256]{1,0:T(8,128)S(1)}, u32[]{:S(2)}, u32[]{:S(2)}) collective-permute-start(f32[24,256]{1,0:T(8,128)S(1)} %reduce_sum.9), channel_id=1, source_target_pairs={{0,2},{2,4},{4,6},{6,0},{1,3},{3,5},{5,7},{7,1},{8,10},{10,12},{12... | collective-permute-start | bytes 73736 | tf_op jit(solution)/shard_map/ppermute | solution.py:207
  123.8 2.0 %collective-permute-done.14 = f32[24,256]{1,0:T(8,128)S(1)} collective-permute-done((f32[24,256]{1,0:T(8,128)S(1)}, f32[24,256]{1,0:T(8,128)S(1)}, u32[]{:S(2)}, u32[]{:S(2)}) %collective-permute-start.14) | collective-permute-done | bytes 24608 | tf_op jit(solution)/shard_map/ppermute | solution.py:207
  125.7 9.2 %all-to-all-done.arrived_ref = f32[32,32,128]{2,1,0:T(8,128)S(1)} async-done(((f32[32,32,128]{2,1,0:T(8,128)}), f32[32,32,128]{2,1,0:T(8,128)S(1)}, u32[]{:S(2)}, u32[]{:S(2)}) %all-to-all-start) | async-done | bytes 524320 | tf_op jit(solution)/shard_map/all_to_all | solution.py:220
  135.8 4.8 %all-to-all-start.3 = ((f32[32,24,256]{2,1,0:T(8,128)}), f32[32,24,256]{2,1,0:T(8,128)S(1)}, u32[]{:S(2)}, u32[]{:S(2)}) async-start(f32[32,24,256]{2,1,0:T(8,128)} %broadcast_in_dim.3), calls=%async_computation.3 | async-start | bytes 1572864 | tf_op jit(solution)/shard_map/all_to_all | solution.py:220
  141.6 21.6 %all-to-all-done.3 = f32[32,24,256]{2,1,0:T(8,128)S(1)} async-done(((f32[32,24,256]{2,1,0:T(8,128)}), f32[32,24,256]{2,1,0:T(8,128)S(1)}, u32[]{:S(2)}, u32[]{:S(2)}) %all-to-all-start.3) | async-done | bytes 786464 | tf_op jit(solution)/shard_map/all_to_all | solution.py:220
  163.1 4.9 %all-to-all-start.1 = ((f32[32,32,128]{2,1,0:T(8,128)}), f32[32,32,128]{2,1,0:T(8,128)S(1)}, u32[]{:S(2)}, u32[]{:S(2)}) async-start(f32[32,32,128]{2,1,0:T(8,128)} %shard_map.41), calls=%async_computation.1 | async-start | bytes 1048576 | tf_op jit(solution)/shard_map/all_to_all | solution.py:220
  168.4 11.9 %shard_map.43.held_ref = bf16[8,4,2,512,256]{4,3,2,1,0:T(8,128)(2,1)} custom-call(f32[4,512,256]{2,1,0:T(8,128)} %refs_1_.3, f32[4,512,256]{2,1,0:T(8,128)} %refs_1_.3, f32[2,512,256]{2,1,0:T(8,128)} %collective-permute-done.1.refs_1_.refs_2_, f32[2,512,256]{2,1,0:T(8,128)} %collective-permute-done.5.refs_1_.refs_3_, ...), custom_call_target="tpu_custom_call" | custom-call | tf_op jit(solution)/shard_map/pallas_call | solution.py:201
  180.3 4.5 %all-to-all-done.1.sums = f32[32,32,128]{2,1,0:T(8,128)S(1)} async-done(((f32[32,32,128]{2,1,0:T(8,128)}), f32[32,32,128]{2,1,0:T(8,128)S(1)}, u32[]{:S(2)}, u32[]{:S(2)}) %all-to-all-start.1) | async-done | bytes 524320 | tf_op jit(solution)/shard_map/all_to_all | solution.py:220
  185.7 10.4 %shard_map.44 = f32[4096,128]{1,0:T(8,128)} custom-call(s32[2]{0:T(128)} %copy-done.5, f32[4096,128]{1,0:T(8,128)} %field_ref.1, f32[4,256,256]{2,1,0:T(8,128)} %factors_ref.3, f32[32,32,128]{2,1,0:T(8,128)} %copy-done.10, f32[768,256]{1,0:T(8,128)} %bitcast.6, f32[768,256]{1,0:T(8,128)} %copy-done.11, bf16[8,4,2,512,256]{4,3,2,1,0:T(8,128)(2,1)} %shard_map.43.held_ref), custom_call_target="tpu_custom_call" | custom-call | tf_op jit(solution)/shard_map/pallas_call | solution.py:201
  (58 shorter events, 15.8 us)
Async XLA Ops:
  1.8 26.4 %collective-permute-start.2 = (f32[2,512,256]{2,1,0:T(8,128)S(1)}, f32[2,512,256]{2,1,0:T(8,128)}, u32[]{:S(2)}, u32[]{:S(2)}) collective-permute-start(f32[2,512,256]{2,1,0:T(8,128)S(1)} %get-tuple-element.9.second_ref), channel_id=1, source_target_pairs={{0,6},{2,0},{4,2},{6,4},{1,7},{3,1},{5,3},{7,5},{8,14},{10,8},{12,... | collective-permute-start | bytes 3145736 | tf_op jit(solution)/shard_map/ppermute | solution.py:207
  4.6 27.3 %collective-permute-start.5 = (f32[2,512,256]{2,1,0:T(8,128)S(1)}, f32[2,512,256]{2,1,0:T(8,128)}, u32[]{:S(2)}, u32[]{:S(2)}) collective-permute-start(f32[2,512,256]{2,1,0:T(8,128)S(1)} %get-tuple-element.9.second_ref), channel_id=1, source_target_pairs={{0,2},{2,4},{4,6},{6,0},{1,3},{3,5},{5,7},{7,1},{8,10},{10,12},{12... | collective-permute-start | bytes 3145736 | tf_op jit(solution)/shard_map/ppermute | solution.py:207
  4.6 48.4 %collective-permute-start.1 = (f32[2,512,256]{2,1,0:T(8,128)S(1)}, f32[2,512,256]{2,1,0:T(8,128)}, u32[]{:S(2)}, u32[]{:S(2)}) collective-permute-start(f32[2,512,256]{2,1,0:T(8,128)S(1)} %get-tuple-element.10.first_ref), channel_id=1, source_target_pairs={{0,2},{2,4},{4,6},{6,0},{1,3},{3,5},{5,7},{7,1},{8,10},{10,12},{12... | collective-permute-start | bytes 3145736 | tf_op jit(solution)/shard_map/ppermute | solution.py:207
  5.4 72.9 %collective-permute-start = (f32[4,512,256]{2,1,0:T(8,128)}, f32[4,512,256]{2,1,0:T(8,128)}, u32[]{:S(2)}, u32[]{:S(2)}) collective-permute-start(f32[4,512,256]{2,1,0:T(8,128)} %refs_1_.3), channel_id=1, source_target_pairs={{0,1},{1,0},{2,3},{3,2},{4,5},{5,4},{6,7},{7,6},{8,9},{9,8},{10,11... | collective-permute-start | bytes 6291464 | tf_op jit(solution)/shard_map/ppermute | solution.py:207
  5.4 48.6 %copy-start.5 = (s32[2]{0:T(128)}, s32[2]{0:T(128)S(1)}, u32[]{:S(2)}) copy-start(s32[2]{0:T(128)S(1)} %pad_add_fusion.place_ref) | copy-start | bytes 28
  10.1 2.5 %collective-permute-start.13 = (f32[768,256]{1,0:T(8,128)S(1)}, f32[768,256]{1,0:T(8,128)S(1)}, u32[]{:S(2)}, u32[]{:S(2)}) collective-permute-start(f32[768,256]{1,0:T(8,128)S(1)} %get-tuple-element.8), channel_id=1, source_target_pairs={{0,1},{1,0},{2,3},{3,2},{4,5},{5,4},{6,7},{7,6},{8,9},{9,8},{10,11... | collective-permute-start | bytes 2359304 | tf_op jit(solution)/shard_map/ppermute | solution.py:207
  12.6 52.8 %collective-permute-start.6 = (f32[2,512,256]{2,1,0:T(8,128)S(1)}, f32[2,512,256]{2,1,0:T(8,128)}, u32[]{:S(2)}, u32[]{:S(2)}) collective-permute-start(f32[2,512,256]{2,1,0:T(8,128)S(1)} %get-tuple-element.10.first_ref), channel_id=1, source_target_pairs={{0,6},{2,0},{4,2},{6,4},{1,7},{3,1},{5,3},{7,5},{8,14},{10,8},{12,... | collective-permute-start | bytes 3145736 | tf_op jit(solution)/shard_map/ppermute | solution.py:207
  28.2 43.9 %collective-permute-start.10 = (f32[2,512,256]{2,1,0:T(8,128)}, f32[2,512,256]{2,1,0:T(8,128)S(1)}, u32[]{:S(2)}, u32[]{:S(2)}) collective-permute-start(f32[2,512,256]{2,1,0:T(8,128)} %collective-permute-done.2.refs_2_.refs_5_), channel_id=1, source_target_pairs={{0,6},{2,0},{4,2},{6,4},{1,7},{3,1},{5,3},{7,5},{8,14},{10,8},{12,... | collective-permute-start | bytes 3145736 | tf_op jit(solution)/shard_map/ppermute | solution.py:207
  32.0 40.1 %collective-permute-start.4 = (f32[2,512,256]{2,1,0:T(8,128)}, f32[2,512,256]{2,1,0:T(8,128)S(1)}, u32[]{:S(2)}, u32[]{:S(2)}) collective-permute-start(f32[2,512,256]{2,1,0:T(8,128)} %collective-permute-done.2.refs_2_.refs_5_), channel_id=1, source_target_pairs={{0,1},{1,0},{2,3},{3,2},{4,5},{5,4},{6,7},{7,6},{8,9},{9,8},{10,11... | collective-permute-start | bytes 3145736 | tf_op jit(solution)/shard_map/ppermute | solution.py:207
  53.0 25.3 %collective-permute-start.9 = (f32[2,512,256]{2,1,0:T(8,128)}, f32[2,512,256]{2,1,0:T(8,128)}, u32[]{:S(2)}, u32[]{:S(2)}) collective-permute-start(f32[2,512,256]{2,1,0:T(8,128)} %collective-permute-done.1.refs_1_.refs_2_), channel_id=1, source_target_pairs={{0,2},{2,4},{4,6},{6,0},{1,3},{3,5},{5,7},{7,1},{8,10},{10,12},{12... | collective-permute-start | bytes 3145736 | tf_op jit(solution)/shard_map/ppermute | solution.py:207
  54.0 51.7 %all-to-all-start.2 = ((f32[32,24,256]{2,1,0:T(8,128)}), f32[32,24,256]{2,1,0:T(8,128)}, u32[]{:S(2)}, u32[]{:S(2)}) async-start(f32[32,24,256]{2,1,0:T(8,128)} %bitcast.4), calls=%async_computation.2 | async-start | bytes 1572864 | tf_op jit(solution)/shard_map/all_to_all | solution.py:220
  65.5 18.6 %collective-permute-start.3 = (f32[2,512,256]{2,1,0:T(8,128)}, f32[2,512,256]{2,1,0:T(8,128)S(1)}, u32[]{:S(2)}, u32[]{:S(2)}) collective-permute-start(f32[2,512,256]{2,1,0:T(8,128)} %collective-permute-done.1.refs_1_.refs_2_), channel_id=1, source_target_pairs={{0,1},{1,0},{2,3},{3,2},{4,5},{5,4},{6,7},{7,6},{8,9},{9,8},{10,11... | collective-permute-start | bytes 3145736 | tf_op jit(solution)/shard_map/ppermute | solution.py:207
  72.1 27.5 %copy-start.1 = (f32[2,512,256]{2,1,0:T(8,128)}, f32[2,512,256]{2,1,0:T(8,128)S(1)}, u32[]{:S(2)}) copy-start(f32[2,512,256]{2,1,0:T(8,128)S(1)} %collective-permute-done.10.refs_2_.refs_7_) | copy-start | bytes 3145732
  72.1 20.2 %collective-permute-start.7 = (f32[2,512,256]{2,1,0:T(8,128)}, f32[2,512,256]{2,1,0:T(8,128)}, u32[]{:S(2)}, u32[]{:S(2)}) collective-permute-start(f32[2,512,256]{2,1,0:T(8,128)} %collective-permute-done.5.refs_1_.refs_3_), channel_id=1, source_target_pairs={{0,1},{1,0},{2,3},{3,2},{4,5},{5,4},{6,7},{7,6},{8,9},{9,8},{10,11... | collective-permute-start | bytes 3145736 | tf_op jit(solution)/shard_map/ppermute | solution.py:207
  72.1 20.2 %collective-permute-start.8 = (f32[2,512,256]{2,1,0:T(8,128)}, f32[2,512,256]{2,1,0:T(8,128)}, u32[]{:S(2)}, u32[]{:S(2)}) collective-permute-start(f32[2,512,256]{2,1,0:T(8,128)} %collective-permute-done.6.refs_2_.refs_4_), channel_id=1, source_target_pairs={{0,1},{1,0},{2,3},{3,2},{4,5},{5,4},{6,7},{7,6},{8,9},{9,8},{10,11... | collective-permute-start | bytes 3145736 | tf_op jit(solution)/shard_map/ppermute | solution.py:207
  78.3 21.2 %collective-permute-start.12 = (f32[2,512,256]{2,1,0:T(8,128)S(1)}, f32[2,512,256]{2,1,0:T(8,128)}, u32[]{:S(2)}, u32[]{:S(2)}) collective-permute-start(f32[2,512,256]{2,1,0:T(8,128)S(1)} %collective-permute-done.10.refs_2_.refs_7_), channel_id=1, source_target_pairs={{0,1},{1,0},{2,3},{3,2},{4,5},{5,4},{6,7},{7,6},{8,9},{9,8},{10,11... | collective-permute-start | bytes 3145736 | tf_op jit(solution)/shard_map/ppermute | solution.py:207
  78.3 21.2 %collective-permute-start.11 = (f32[2,512,256]{2,1,0:T(8,128)}, f32[2,512,256]{2,1,0:T(8,128)}, u32[]{:S(2)}, u32[]{:S(2)}) collective-permute-start(f32[2,512,256]{2,1,0:T(8,128)} %collective-permute-done.9.refs_1_.refs_6_), channel_id=1, source_target_pairs={{0,1},{1,0},{2,3},{3,2},{4,5},{5,4},{6,7},{7,6},{8,9},{9,8},{10,11... | collective-permute-start | bytes 3145736 | tf_op jit(solution)/shard_map/ppermute | solution.py:207
  105.7 29.2 %all-to-all-start = ((f32[32,32,128]{2,1,0:T(8,128)}), f32[32,32,128]{2,1,0:T(8,128)S(1)}, u32[]{:S(2)}, u32[]{:S(2)}) async-start(f32[32,32,128]{2,1,0:T(8,128)} %copy-done.3), calls=%async_computation | async-start | bytes 1048576 | tf_op jit(solution)/shard_map/all_to_all | solution.py:220
  118.3 3.9 %collective-permute-start.16 = (f32[24,256]{1,0:T(8,128)S(1)}, f32[24,256]{1,0:T(8,128)S(1)}, u32[]{:S(2)}, u32[]{:S(2)}) collective-permute-start(f32[24,256]{1,0:T(8,128)S(1)} %reduce_sum.9), channel_id=1, source_target_pairs={{0,6},{2,0},{4,2},{6,4},{1,7},{3,1},{5,3},{7,5},{8,14},{10,8},{12,... | collective-permute-start | bytes 73736 | tf_op jit(solution)/shard_map/ppermute | solution.py:207
  118.4 5.4 %collective-permute-start.15 = (f32[24,256]{1,0:T(8,128)S(1)}, f32[24,256]{1,0:T(8,128)S(1)}, u32[]{:S(2)}, u32[]{:S(2)}) collective-permute-start(f32[24,256]{1,0:T(8,128)S(1)} %reduce_sum.9), channel_id=1, source_target_pairs={{0,2},{2,4},{4,6},{6,0},{1,3},{3,5},{5,7},{7,1},{8,10},{10,12},{12... | collective-permute-start | bytes 73736 | tf_op jit(solution)/shard_map/ppermute | solution.py:207
  120.4 5.3 %collective-permute-start.14 = (f32[24,256]{1,0:T(8,128)S(1)}, f32[24,256]{1,0:T(8,128)S(1)}, u32[]{:S(2)}, u32[]{:S(2)}) collective-permute-start(f32[24,256]{1,0:T(8,128)S(1)} %reduce_sum.9), channel_id=1, source_target_pairs={{0,4},{2,6},{4,0},{6,2},{1,5},{3,7},{5,1},{7,3},{8,12},{10,14},{12... | collective-permute-start | bytes 73736 | tf_op jit(solution)/shard_map/ppermute | solution.py:207
  135.8 27.3 %all-to-all-start.3 = ((f32[32,24,256]{2,1,0:T(8,128)}), f32[32,24,256]{2,1,0:T(8,128)S(1)}, u32[]{:S(2)}, u32[]{:S(2)}) async-start(f32[32,24,256]{2,1,0:T(8,128)} %broadcast_in_dim.3), calls=%async_computation.3 | async-start | bytes 1572864 | tf_op jit(solution)/shard_map/all_to_all | solution.py:220
  163.1 21.7 %all-to-all-start.1 = ((f32[32,32,128]{2,1,0:T(8,128)}), f32[32,32,128]{2,1,0:T(8,128)S(1)}, u32[]{:S(2)}, u32[]{:S(2)}) async-start(f32[32,32,128]{2,1,0:T(8,128)} %shard_map.41), calls=%async_computation.1 | async-start | bytes 1048576 | tf_op jit(solution)/shard_map/all_to_all | solution.py:220
  168.1 12.2 %collective-permute-start.17 = (f32[768,256]{1,0:T(8,128)S(1)}, f32[768,256]{1,0:T(8,128)S(1)}, u32[]{:S(2)}, u32[]{:S(2)}) collective-permute-start(f32[768,256]{1,0:T(8,128)S(1)} %bitcast.5), channel_id=1, source_target_pairs={{0,1},{1,0},{2,3},{3,2},{4,5},{5,4},{6,7},{7,6},{8,9},{9,8},{10,11... | collective-permute-start | bytes 2359304 | tf_op jit(solution)/shard_map/ppermute | solution.py:207
  (10 other events, 57.4 us)
